TPU v7x, 32 devices: a whole 2x2x4 slice. The times are simulated.
32 devices in a mesh: tm: 4 (over z), batch: 4 (over x, core), width: 2 (over y).
Axes of the slice: x: 2, y: 2, z: 4, core: 2. Of those that a mesh axis runs over, the one named last changes fastest.
Arguments:
- moves: int32 [8, 1024], P('batch', 'tm'), may hold values from 0 to 361
- lengths: int32 [8], P('batch'), may hold values from 1 to 1024
- outcomes: int32 [8], P('batch'), may hold values from -1 to 1
- embedded: bfloat16 [8, 1024, 2048], P('batch', 'tm', 'width'), may hold values from -6 to 6
- w_branches: bfloat16 [4, 2048, 2048], P(None, ('tm', 'batch'), 'width'), may hold values from -0.125 to 0.125
- conv_w: float32 [4, 2048], P(None, 'width'), may hold values from -3 to 3
- gate_bias: float32 [2, 2048], P(None, 'width'), may hold values from -4 to 4
- rates: float32 [2048], P('width'), may hold values from 0.001 to 0.105
- w_down: bfloat16 [2048, 2048], P(('tm', 'batch'), 'width'), may hold values from -0.125 to 0.125
- w_policy: bfloat16 [2048, 362], P('width'), may hold values from -12 to 12
- w_value: bfloat16 [2048], P('width'), may hold values from -0.125 to 0.125
Outputs:
- position_loss: float32 [8, 1024], P('batch', 'tm')
- value: float32 [8, 1024], P('batch', 'tm')
All inputs are finite; a program needn't handle non-finite values.
Results may differ from a plain program's by a relative error of at most 0.0033.
Values may be sent and summed in bfloat16 or wider, within the bound.
A program may use at most 128 MiB of HBM per device.

v0:
```python
import jax
import jax.numpy as jnp
from jax import lax
from jax.sharding import PartitionSpec as P

D = 2048
KERNEL = 4


def from_behind(value, axis, steps):
    count = lax.axis_size(axis)
    initial, last = (max(0, -steps), min(count, count - steps))
    return lax.ppermute(value, axis, [(source, source + steps) for source in range(initial, last)])


def link(early, late):
    return (early[0] + late[0], jnp.exp(late[0]) * early[1] + late[1])


def shards(
    moves,
    lengths,
    outcomes,
    embedded,
    w_branches,
    conv_w,
    gate_bias,
    rates,
    w_down,
    w_policy,
    w_value,
):
    games, block_len, half = embedded.shape
    count = games * block_len
    chans = w_branches.shape[2]
    features = lax.all_gather(embedded, "width", axis=2, tiled=True).reshape(count, -1)
    proj = jnp.einsum(
        "td,kdn->ktn",
        features,
        lax.all_gather(w_branches, ("tm", "batch"), axis=1, tiled=True),
        preferred_element_type=jnp.float32,
    )
    proj = proj.reshape(4, games, block_len, chans)
    gated = jax.nn.gelu(proj[0])
    source = proj[1]
    prior = from_behind(source[:, block_len - (KERNEL - 1) :, :], "tm", 1)
    extended = jnp.concatenate([prior, source], 1)
    conv = jnp.zeros((games, block_len, chans), jnp.float32)
    for k in range(KERNEL):
        conv = conv + conv_w[k] * extended[:, KERNEL - 1 - k : KERNEL - 1 - k + block_len]
    recur = jax.nn.sigmoid(proj[2] + gate_bias[0])
    inflow = jax.nn.sigmoid(proj[3] + gate_bias[1])
    log_a = -8.0 * recur * rates
    decay = jnp.exp(log_a)
    drive = jnp.sqrt(1.0 - decay * decay) * inflow * conv
    summed, local = lax.associative_scan(link, (log_a, drive), axis=1)
    block_decay = jnp.exp(summed[:, -1])
    block_end = local[:, -1]

    def relay(step, state):
        outgoing, _ = state
        arrived = from_behind(outgoing, "tm", 1)
        return (block_decay * arrived + block_end, arrived)

    _, incoming = lax.fori_loop(
        0, lax.axis_size("tm") - 1, relay, (block_end, jnp.zeros_like(block_end))
    )
    hidden = local + jnp.exp(summed) * incoming[:, None, :]
    mixed = (hidden * gated).astype(jnp.bfloat16).reshape(count, chans)
    partial_down = lax.dot_general(
        mixed,
        lax.all_gather(w_down, ("tm", "batch"), axis=0, tiled=True),
        (((1,), (1,)), ((), ())),
        preferred_element_type=jnp.float32,
    )
    down = lax.psum_scatter(partial_down, "width", scatter_dimension=1, tiled=True)
    resid = (embedded.reshape(count, half).astype(jnp.float32) + down).astype(jnp.bfloat16)
    wide = resid.astype(jnp.float32)
    local_sq = jnp.sum(wide * wide, -1)
    local_logits = jnp.dot(resid, w_policy, preferred_element_type=jnp.float32)
    local_value = jnp.dot(resid, w_value, preferred_element_type=jnp.float32)
    raw_logits, raw_value, sumsq = lax.psum((local_logits, local_value, local_sq), "width")
    norm = lax.rsqrt(sumsq / D + 1e-06)
    logits = raw_logits * norm[:, None]
    value = jnp.tanh(raw_value * norm)
    top = jnp.max(logits, -1, keepdims=True)
    lse = top[:, 0] + jnp.log(jnp.sum(jnp.exp(logits - top), -1))
    column = lax.broadcasted_iota(jnp.int32, logits.shape, 1)
    picked = jnp.sum(jnp.where(column == moves.reshape(count, 1), logits, 0.0), -1)
    target = jnp.broadcast_to(outcomes.astype(jnp.float32)[:, None], (games, block_len)).reshape(
        count
    )
    position = lax.axis_index("tm") * block_len + lax.broadcasted_iota(
        jnp.int32, (games, block_len), 1
    )
    where_live = (position < lengths[:, None]).reshape(count)
    loss = jnp.where(where_live, lse - picked + (value - target) ** 2, 0.0)
    return (loss.reshape(games, block_len), value.reshape(games, block_len))


def solution(mesh):
    in_specs = (
        P("batch", "tm"),
        P("batch"),
        P("batch"),
        P("batch", "tm", "width"),
        P(None, ("tm", "batch"), "width"),
        P(None, "width"),
        P(None, "width"),
        P("width"),
        P(("tm", "batch"), "width"),
        P("width", None),
        P("width"),
    )
    out_specs = (P("batch", "tm"), P("batch", "tm"))
    return jax.shard_map(shards, mesh=mesh, in_specs=in_specs, out_specs=out_specs, check_vma=False)
```

profile of v0, /device:TPU:0, one launch (start us, length us, event | category | flops | bytes accessed | tf_op | source)
XLA Modules:
  0.0 492.6 jit_solution(15699372225943647497)
XLA Ops:
  9.5 35.9 %all-gather.6.cloned.1.call-done = bf16[2,256,2048]{2,1,0:T(8,128)(2,1)} async-done(((bf16[2,256,1024]{2,1,0:T(8,128)(2,1)}), bf16[2,256,2048]{2,1,0:T(8,128)(2,1)}) %all-gather.6.cloned.1.call-update) | async-done | bytes 2097168 | tf_op jit(solution)/shard_map/all_gather | solution.py:36
  45.4 128.7 %all-gather.4.cloned.1.call-done = bf16[4,2048,1024]{2,1,0:T(8,128)(2,1)} async-done(((bf16[4,128,1024]{2,1,0:T(8,128)(2,1)}), bf16[4,2048,1024]{2,1,0:T(8,128)(2,1)}) %all-gather.4.cloned.1.call-update) | async-done | bytes 16777232 | tf_op jit(solution)/shard_map/all_gather | solution.py:40
  174.1 12.5 %convolution_bitcast_fusion = f32[4,512,1024]{2,1,0:T(8,128)S(1)} fusion(bf16[512,2048,1]{1,0,2:T(8,128)(2,1)} %bitcast.75, bf16[4,2048,1024]{2,1,0:T(8,128)(2,1)} %all-gather.4.cloned.1.call-done), kind=kOutput, calls=%fused_computation.1 | convolution fusion | flops 8589934592 | bytes 27262976 | tf_op jit(solution)/shard_map/td,kdn->ktn/dot_general | solution.py:37
  186.6 2.9 fusion.30
  194.2 7.6 %fusion.4 = (f32[2,256,1024]{2,1,0:T(8,128)S(1)}, f32[2,256,1024]{2,1,0:T(8,128)}) fusion(f32[2,3,1024]{2,1,0:T(4,128)S(1)} %collective-permute-done.1, f32[2,256,1024]{2,1,0:T(8,128)} %bitcast.47, f32[2,256,1024]{2,1,0:T(8,128)} %bitcast.50, f32[1024]{0:T(1024)S(1)} %bitcast.69, f32[1024]{0:T(1024)S(1)} %bitcast.70, f32[1024]{0:T(1024)S(1)} %bitcast.68, ...), kind=kLoop, calls=%fused_computation.9 | loop fusion | flops 12058624 | bytes 10539008 | tf_op jit(solution)/shard_map/mul | solution.py:55
  201.7 2.9 slice.298
  204.6 2.9 slice.299
  207.5 5.4 %slice.297 = f32[2,128,1024]{2,1,0:T(8,128)} slice(f32[2,256,1024]{2,1,0:T(8,128)} %get-tuple-element.48), slice={[0:2:1], [1:256:2], [0:1024:1]} | slice | bytes 2097152 | tf_op jit(solution)/shard_map/slice | solution.py:56
  212.9 5.5 %slice.301 = f32[2,128,1024]{2,1,0:T(8,128)} slice(f32[2,256,1024]{2,1,0:T(8,128)} %get-tuple-element.48), slice={[0:2:1], [0:255:2], [0:1024:1]} | slice | bytes 2097152 | tf_op jit(solution)/shard_map/slice | solution.py:56
  218.4 4.2 multiply_add_fusion.1
  222.5 3.3 slice.304
  225.8 3.3 slice.305
  229.1 3.3 slice.303
  232.3 3.2 slice.307
  290.1 3.3 slice.302
  293.4 3.3 slice.351
  299.6 5.6 %slice.296 = f32[2,127,1024]{2,1,0:T(8,128)} slice(f32[2,256,1024]{2,1,0:T(8,128)} %get-tuple-element.48), slice={[0:2:1], [2:256:2], [0:1024:1]} | slice | bytes 2080768 | tf_op jit(solution)/shard_map/slice | solution.py:56
  305.2 3.0 slice.353
  318.5 5.5 %pad.129 = f32[2,256,1024]{2,1,0:T(8,128)} pad(f32[2,128,1024]{2,1,0:T(8,128)} %add.338, f32[]{:T(128)} %constant.6.clone.1), padding=0_0_0x1_0_1x0_0_0 | pad | bytes 3145732 | tf_op jit(solution)/shard_map/pad | solution.py:56
  325.8 3.0 pad.110
  337.8 5.4 %pad.128 = f32[2,256,1024]{2,1,0:T(8,128)} pad(f32[2,128,1024]{2,1,0:T(8,128)} %pad_maximum_fusion.2, f32[]{:T(128)} %constant.6.clone.1), padding=0_0_0x0_1_1x0_0_0 | pad | bytes 3145732 | tf_op jit(solution)/shard_map/pad | solution.py:56
  344.1 5.5 %pad.113 = f32[2,256,1024]{2,1,0:T(8,128)} pad(f32[2,128,1024]{2,1,0:T(8,128)} %add.322, f32[]{:T(128)} %constant.6.clone.1), padding=0_0_0x1_0_1x0_0_0 | pad | bytes 3145732 | tf_op jit(solution)/shard_map/pad | solution.py:56
  351.9 5.5 %pad.112 = f32[2,256,1024]{2,1,0:T(8,128)} pad(f32[2,128,1024]{2,1,0:T(8,128)} %pad_maximum_fusion.1, f32[]{:T(128)} %constant.6.clone.1), padding=0_0_0x0_1_1x0_0_0 | pad | bytes 3145732 | tf_op jit(solution)/shard_map/pad | solution.py:56
  358.4 18.6 %while.12 = (s32[]{:T(128)}, f32[2,1024]{1,0:T(2,128)S(1)}, f32[2,1024]{1,0:T(2,128)}, f32[2,1024]{1,0:T(2,128)S(1)}, f32[2,1024]{1,0:T(2,128)S(1)}, /*index=5*/s32[]{:T(128)}) while((s32[]{:T(128)}, f32[2,1024]{1,0:T(2,128)S(1)}, f32[2,1024]{1,0:T(2,128)}, f32[2,1024]{1,0:T(2,128)S(1)}, f32[2,1024]{1,0:T(2,128)S(1)}, ...), condition=%wide.region_1.0_spmd, body=%wide.region_0.0_spmd.sunk | while | flops 4098 | bytes 98441 | solution.py:65
  358.4 4.4 collective-permute-start
  364.7 4.2 collective-permute-start
  370.8 4.2 collective-permute-start
  377.0 5.8 %fusion.16 = bf16[2,256,1024]{2,1,0:T(8,128)(2,1)} fusion(f32[2,256,1024]{2,1,0:T(8,128)} %bitcast.48, f32[2,256,1024]{2,1,0:T(8,128)} %pad.128, f32[2,256,1024]{2,1,0:T(8,128)S(1)} %copy-done.4, f32[2,256,1024]{2,1,0:T(8,128)} %pad.112, f32[2,256,1024]{2,1,0:T(8,128)} %pad.113, f32[2,1024]{1,0:T(2,128)} %get-tuple-element.28), kind=kLoop, calls=%fused_computation.21 | loop fusion | flops 7340032 | bytes 11542528 | tf_op jit(solution)/shard_map/convert_element_type | solution.py:69
  382.8 6.9 %fusion.35 = f32[512,2048]{1,0:T(8,128)} fusion(bf16[512,1024]{1,0:T(8,128)(2,1)} %bitcast.51, bf16[2048,1024]{1,0:T(8,128)(2,1)} %all-gather.8.cloned.1.call-done), kind=kOutput, calls=%fused_computation.100 | convolution fusion | flops 2147483648 | bytes 9437184 | tf_op jit(solution)/shard_map/dot_general | solution.py:70
  389.7 55.3 %reduce-scatter.2.cloned.1.call-done = f32[512,1024]{1,0:T(8,128)} async-done(((f32[512,2048]{1,0:T(8,128)}), f32[512,1024]{1,0:T(8,128)}) %reduce-scatter.2.cloned.1.call-update) | async-done | bytes 2097168 | tf_op jit(solution)/shard_map/reduce_scatter | solution.py:76
  449.1 4.9 all-reduce.32
  454.1 28.3 %all-reduce.35.cloned.1.call-done = f32[512,362]{0,1:T(8,128)} async-done(((f32[512,362]{0,1:T(8,128)}), f32[512,362]{0,1:T(8,128)}) %all-reduce.35.cloned.1.call-update) | async-done | bytes 741392 | tf_op jit(solution)/shard_map/psum | solution.py:82
  (233 shorter events, 102.8 us)
Async XLA Ops:
  7.2 439.9 %copy-start = (bf16[1024,362]{0,1:T(8,128)(2,1)S(1)}, bf16[1024,362]{0,1:T(8,128)(2,1)}, u32[]{:S(2)}) copy-start(bf16[1024,362]{0,1:T(8,128)(2,1)} %param.22) | copy-start | bytes 2224132
  7.2 2.3 copy-start.34
  7.2 38.2 %all-gather.6.cloned.1.call-start = ((), (), s32[]{:S(2)}) async-start(), calls=%async_computation.2 | async-start | bytes 3145728 | tf_op jit(solution)/shard_map/all_gather | solution.py:36
  7.9 166.1 %all-gather.4.cloned.1.call-start = ((), (), s32[]{:S(2)}) async-start(), calls=%async_computation.1 | async-start | bytes 17825792 | tf_op jit(solution)/shard_map/all_gather | solution.py:40
  8.7 374.1 %all-gather.8.cloned.1.call-start = ((), (), s32[]{:S(2)}) async-start(), calls=%async_computation.3 | async-start | bytes 4456448 | tf_op jit(solution)/shard_map/all_gather | solution.py:72
  9.4 435.6 %reduce-scatter.2.cloned.1.call-start = ((), (), s32[]{:S(2)}) async-start(), calls=%async_computation.4 | async-start | bytes 6291456 | tf_op jit(solution)/shard_map/reduce_scatter | solution.py:76
  186.6 6.1 %copy-start.35 = (f32[1024]{0:T(1024)S(1)}, f32[1024]{0:T(1024)}, u32[]{:S(2)}) copy-start(f32[1024]{0:T(1024)} %param.20) | copy-start | bytes 12292
  190.9 3.3 collective-permute-start.1
  299.6 10.6 %copy-start.18 = (f32[2,2,1024]{2,1,0:T(2,128)S(1)}, f32[2,2,1024]{2,1,0:T(2,128)}, u32[]{:S(2)}) copy-start(f32[2,2,1024]{2,1,0:T(2,128)} %slice.335) | copy-start | bytes 49156
  299.6 10.6 %copy-start.19 = (f32[2,2,1024]{2,1,0:T(2,128)S(1)}, f32[2,2,1024]{2,1,0:T(2,128)}, u32[]{:S(2)}) copy-start(f32[2,2,1024]{2,1,0:T(2,128)} %slice.333) | copy-start | bytes 49156
  299.6 10.6 %copy-start.20 = (f32[2,2,1024]{2,1,0:T(2,128)S(1)}, f32[2,2,1024]{2,1,0:T(2,128)}, u32[]{:S(2)}) copy-start(f32[2,2,1024]{2,1,0:T(2,128)} %slice.337) | copy-start | bytes 49156
  299.6 10.8 %copy-start.15 = (f32[1,8,1024]{2,1,0:T(8,128)S(1)}, f32[1,8,1024]{2,1,0:T(8,128)}, u32[]{:S(2)}) copy-start(f32[1,8,1024]{2,1,0:T(8,128)} %get-tuple-element.103) | copy-start | bytes 98308
  299.6 11.1 %copy-start.16 = (f32[2,3,1024]{2,1,0:T(4,128)S(1)}, f32[2,3,1024]{2,1,0:T(4,128)}, u32[]{:S(2)}) copy-start(f32[2,3,1024]{2,1,0:T(4,128)} %slice.326) | copy-start | bytes 73732
  299.6 11.1 %copy-start.17 = (f32[2,3,1024]{2,1,0:T(4,128)S(1)}, f32[2,3,1024]{2,1,0:T(4,128)}, u32[]{:S(2)}) copy-start(f32[2,3,1024]{2,1,0:T(4,128)} %slice.343) | copy-start | bytes 73732
  305.2 5.6 %copy-start.32 = (f32[2,1,1024]{2,1,0:T(1,128)S(1)}, f32[2,1,1024]{2,1,0:T(1,128)}, u32[]{:S(2)}) copy-start(f32[2,1,1024]{2,1,0:T(1,128)} %slice.411) | copy-start | bytes 24580
  305.2 5.7 %copy-start.31 = (f32[2,1,1024]{2,1,0:T(1,128)S(1)}, f32[2,1,1024]{2,1,0:T(1,128)}, u32[]{:S(2)}) copy-start(f32[2,1,1024]{2,1,0:T(1,128)} %slice.385) | copy-start | bytes 24580
  305.2 5.8 %copy-start.13 = (f32[2,7,1024]{2,1,0:T(8,128)S(1)}, f32[2,7,1024]{2,1,0:T(8,128)}, u32[]{:S(2)}) copy-start(f32[2,7,1024]{2,1,0:T(8,128)} %slice.320) | copy-start | bytes 172036
  305.2 5.8 %copy-start.14 = (f32[2,7,1024]{2,1,0:T(8,128)S(1)}, f32[2,7,1024]{2,1,0:T(8,128)}, u32[]{:S(2)}) copy-start(f32[2,7,1024]{2,1,0:T(8,128)} %slice.345) | copy-start | bytes 172036
  305.2 5.9 %copy-start.30 = (f32[2,1,1024]{2,1,0:T(1,128)S(1)}, f32[2,1,1024]{2,1,0:T(1,128)}, u32[]{:S(2)}) copy-start(f32[2,1,1024]{2,1,0:T(1,128)} %slice.410) | copy-start | bytes 24580
  308.2 3.1 copy-start.29
  318.5 5.5 %copy-start.23 = (f32[2,1,1024]{2,1,0:T(1,128)S(1)}, f32[2,1,1024]{2,1,0:T(1,128)}, u32[]{:S(2)}) copy-start(f32[2,1,1024]{2,1,0:T(1,128)} %slice.381) | copy-start | bytes 24580
  330.9 2.9 copy-start.1
  330.9 2.9 copy-start.2
  330.9 2.9 copy-start.6
  333.7 2.9 copy-start.22
  337.8 5.4 %copy-start.4 = (f32[2,256,1024]{2,1,0:T(8,128)S(1)}, f32[2,256,1024]{2,1,0:T(8,128)}, u32[]{:S(2)}) copy-start(f32[2,256,1024]{2,1,0:T(8,128)} %pad.129) | copy-start | bytes 6291460
  343.2 6.4 %copy-start.21 = (f32[2,1,1024]{2,1,0:T(1,128)S(1)}, f32[2,1,1024]{2,1,0:T(1,128)}, u32[]{:S(2)}) copy-start(f32[2,1,1024]{2,1,0:T(1,128)} %slice.380) | copy-start | bytes 24580
  358.4 5.7 %collective-permute-start = (f32[2,1024]{1,0:T(2,128)S(1)}, f32[2,1024]{1,0:T(2,128)S(1)}, u32[]{:S(2)}, u32[]{:S(2)}) collective-permute-start(f32[2,1024]{1,0:T(2,128)S(1)} %get-tuple-element.135), channel_id=1, source_target_pairs={{0,8},{8,16},{16,24},{1,9},{9,17},{17,25},{2,10},{10,18},{18,26},{... | collective-permute-start | bytes 24584 | tf_op jit(solution)/shard_map/while/body/eval_jaxpr/ppermute | solution.py:13
  364.7 5.5 %collective-permute-start = (f32[2,1024]{1,0:T(2,128)S(1)}, f32[2,1024]{1,0:T(2,128)S(1)}, u32[]{:S(2)}, u32[]{:S(2)}) collective-permute-start(f32[2,1024]{1,0:T(2,128)S(1)} %get-tuple-element.135), channel_id=1, source_target_pairs={{0,8},{8,16},{16,24},{1,9},{9,17},{17,25},{2,10},{10,18},{18,26},{... | collective-permute-start | bytes 24584 | tf_op jit(solution)/shard_map/while/body/eval_jaxpr/ppermute | solution.py:13
  370.8 5.5 %collective-permute-start = (f32[2,1024]{1,0:T(2,128)S(1)}, f32[2,1024]{1,0:T(2,128)S(1)}, u32[]{:S(2)}, u32[]{:S(2)}) collective-permute-start(f32[2,1024]{1,0:T(2,128)S(1)} %get-tuple-element.135), channel_id=1, source_target_pairs={{0,8},{8,16},{16,24},{1,9},{9,17},{17,25},{2,10},{10,18},{18,26},{... | collective-permute-start | bytes 24584 | tf_op jit(solution)/shard_map/while/body/eval_jaxpr/ppermute | solution.py:13
  389.6 55.4 %copy-start.5 = (bf16[2,256,1024]{2,1,0:T(8,128)(2,1)S(1)}, bf16[2,256,1024]{2,1,0:T(8,128)(2,1)}, u32[]{:S(2)}) copy-start(bf16[2,256,1024]{2,1,0:T(8,128)(2,1)} %param.16) | copy-start | bytes 3145732
  389.7 92.7 %all-reduce.35.cloned.1.call-start = ((), (), s32[]{:S(2)}) async-start(), calls=%async_computation.5 | async-start | bytes 1507328 | tf_op jit(solution)/shard_map/psum | solution.py:82
  (19 other events, 21.4 us)
Sparse Core Ops, SparseCore 0:
  9.6 35.8 all-gather.5
  47.6 126.4 all-gather.3
  176.2 48.9 all-gather.7
  389.8 55.1 reduce-scatter.1
  448.7 33.6 all-reduce.34
where the time goes:
time: 496 us; the launch traced here: 493 us
  waiting for transfers between devices  256 us (52%)
  local copies, waits for them, and re-layouts  133 us (27%)
  other arithmetic  48.4 us (10%)
  matrix products  21.2 us (4%)
  starting transfers between devices  14.7 us (3%)
  between operations  14.6 us (3%)
    all_gather x1, waiting for transfers between devices, shards(): lax.all_gather(w_branches, ('tm', 'batch'), axis=1, tiled=True)  129 us
    slice x52, local copies, waits for them, and re-layouts, shards(): summed, local = lax.associative_scan(link, (log_a, drive), axis=1)  94.9 us
    reduce_scatter x1, waiting for transfers between devices, shards(): lax.psum_scatter(partial_down, 'width', scatter_dimension=1, tiled=True)  55.3 us
    all_gather x1, waiting for transfers between devices, shards(): lax.all_gather(embedded, 'width', axis=2, tiled=True).reshape(count, -1)  35.9 us
    pad x28, local copies, waits for them, and re-layouts, shards(): summed, local = lax.associative_scan(link, (log_a, drive), axis=1)  29.4 us
    psum x1, waiting for transfers between devices, shards(): lax.psum((local_logits, local_value, local_sq), 'width')  28.3 us
    add x13, other arithmetic, link(): return (early[0] + late[0], jnp.exp(late[0]) * early[1] + late[1])  17.8 us
    ppermute x4, starting transfers between devices, from_behind(): lax.ppermute(value, axis, [(source, source + steps) for source in range(i...  14.6 us
  transfers between devices with their start and end apart: 9, of which 8 were waited for; matrix products, arithmetic and copies ran while one was open for 37% of the time, Pallas kernels for 0%

commit v1 on v0

v1 whole, which is shorter than its diff:
```python
import functools

import jax
import jax.numpy as jnp
from jax import lax
from jax.experimental import pallas as pl
from jax.experimental.pallas import tpu as pltpu
from jax.sharding import PartitionSpec as P

KERNEL = 4
SUB = 8


def swap(value, axis):
    n = lax.axis_size(axis)
    return lax.ppermute(value, axis, [(i, n - 1 - i) for i in range(n)])


def from_behind(value, axis):
    n = lax.axis_size(axis)
    return lax.ppermute(value, axis, [(i, i + 1) for i in range(n - 1)])


def interleave(x):
    games, steps = x.shape[:2]
    return jnp.swapaxes(x.reshape(games, SUB, steps // SUB, *x.shape[2:]), 1, 2).reshape(x.shape)


def restore(x):
    games, steps = x.shape[:2]
    return jnp.swapaxes(x.reshape(games, steps // SUB, SUB, *x.shape[2:]), 1, 2).reshape(x.shape)


def both(own, other, axis, dim):
    first = lax.axis_index(axis) == 0
    return jnp.concatenate([jnp.where(first, own, other), jnp.where(first, other, own)], dim)


def scan_kernel(
    proj, halo, conv_w, bias, rates, hg, pg, ends, h_s, p_s, g_s, carry_s
):
    steps, cols = proj.shape[1], proj.shape[2]
    seg = steps // SUB
    w = [conv_w[k : k + 1, :] for k in range(KERNEL)]
    b0, b1 = bias[0:1, :], bias[1:2, :]
    scale = -8.0 * rates[0:1, :]
    row = lax.broadcasted_iota(jnp.int32, (SUB, cols), 0)

    def rows(k, t):
        return proj[k, pl.ds(pl.multiple_of(t * SUB, SUB), SUB), :]

    def before(j):
        rolled = pltpu.roll(rows(1, seg - j), 1, 0)
        return jnp.where(row == 0, halo[0, KERNEL - 1 - j : KERNEL - j, :], rolled)

    def step(t, state):
        h, p, x1, x2, x3 = state
        x0 = rows(1, t)
        conv = w[0] * x0 + w[1] * x1 + w[2] * x2 + w[3] * x3
        recur = jax.nn.sigmoid(rows(2, t) + b0)
        inflow = jax.nn.sigmoid(rows(3, t) + b1)
        a = jnp.exp(recur * scale)
        h = a * h + jnp.sqrt(1.0 - a * a) * inflow * conv
        p = a * p
        h_s[t] = h
        p_s[t] = p
        g_s[t] = jax.nn.gelu(rows(0, t))
        return h, p, x0, x1, x2

    zero = jnp.zeros((SUB, cols), jnp.float32)
    h, p, _, _, _ = lax.fori_loop(
        0, seg, step, (zero, zero + 1.0, before(1), before(2), before(3)), unroll=4
    )
    run, dec = jnp.zeros((1, cols), jnp.float32), jnp.ones((1, cols), jnp.float32)
    for s in range(SUB):
        carry_s[0, s : s + 1, :] = run
        carry_s[1, s : s + 1, :] = dec
        run = p[s : s + 1] * run + h[s : s + 1]
        dec = p[s : s + 1] * dec
    ends[0, 0:1, :] = run
    ends[0, 1:2, :] = dec
    run, dec = carry_s[0], carry_s[1]

    def finish(t, _):
        g, p = g_s[t], p_s[t]
        hg[pl.ds(pl.multiple_of(t * SUB, SUB), SUB), :] = (h_s[t] + p * run) * g
        pg[pl.ds(pl.multiple_of(t * SUB, SUB), SUB), :] = p * dec * g
        return 0

    lax.fori_loop(0, seg, finish, 0, unroll=4)


def block_scan(proj, halo, conv_w, gate_bias, rates, games):
    _, count, chans = proj.shape
    steps = count // games
    cols = min(512, chans)
    return pl.pallas_call(
        scan_kernel,
        grid=(games, chans // cols),
        in_specs=[
            pl.BlockSpec((4, steps, cols), lambda g, c: (0, g, c)),
            pl.BlockSpec((1, KERNEL - 1, cols), lambda g, c: (g, 0, c)),
            pl.BlockSpec((KERNEL, cols), lambda g, c: (0, c)),
            pl.BlockSpec((2, cols), lambda g, c: (0, c)),
            pl.BlockSpec((1, cols), lambda g, c: (0, c)),
        ],
        out_specs=[
            pl.BlockSpec((steps, cols), lambda g, c: (g, c)),
            pl.BlockSpec((steps, cols), lambda g, c: (g, c)),
            pl.BlockSpec((1, 2, cols), lambda g, c: (g, 0, c)),
        ],
        out_shape=[
            jax.ShapeDtypeStruct((count, chans), jnp.float32),
            jax.ShapeDtypeStruct((count, chans), jnp.float32),
            jax.ShapeDtypeStruct((games, 2, chans), jnp.float32),
        ],
        scratch_shapes=[pltpu.VMEM((steps // SUB, SUB, cols), jnp.float32)] * 3
        + [pltpu.VMEM((2, SUB, cols), jnp.float32)],
        cost_estimate=pl.CostEstimate(
            flops=60 * count * chans, bytes_accessed=24 * count * chans, transcendentals=8 * count * chans
        ),
    )(proj, halo, conv_w, gate_bias, rates.reshape(1, chans))


def shards(
    moves,
    lengths,
    outcomes,
    embedded,
    w_branches,
    conv_w,
    gate_bias,
    rates,
    w_down,
    w_policy,
    w_value,
):
    games, block_len, half = embedded.shape
    count = games * block_len
    chans = w_branches.shape[2]
    n_width = lax.axis_size("width")
    me = lax.axis_index("width")
    own_rows = count // n_width

    flat = interleave(embedded).reshape(count, half)
    features = both(flat, swap(flat, "width"), "width", 1)
    heads = jnp.concatenate([w_policy, w_value[:, None]], 1)
    heads = both(heads, swap(heads, "width"), "width", 0)
    depth = features.shape[1]
    tail = features.reshape(games, block_len // SUB, SUB, depth)[:, 1 - KERNEL :, SUB - 1, :]
    tail = from_behind(tail, "tm").reshape(games * (KERNEL - 1), depth)

    w_full = lax.all_gather(w_branches, ("tm", "batch"), axis=1, tiled=True)
    proj = jnp.einsum("td,kdn->ktn", features, w_full, preferred_element_type=jnp.float32)
    halo = jnp.dot(tail, w_full[1], preferred_element_type=jnp.float32)
    hg, pg, ends = block_scan(
        proj, halo.reshape(games, KERNEL - 1, chans), conv_w, gate_bias, rates, games
    )
    w_out = lax.all_gather(w_down, ("tm", "batch"), axis=0, tiled=True)
    ends_all = lax.all_gather(ends, "tm", axis=0)
    state = jnp.zeros((games, chans), jnp.float32)
    here = lax.axis_index("tm")
    for j in range(lax.axis_size("tm") - 1):
        state = jnp.where(j < here, ends_all[j, :, 1] * state + ends_all[j, :, 0], state)
    mixed = hg.reshape(games, block_len, chans) + pg.reshape(games, block_len, chans) * state[:, None]
    mixed = mixed.astype(jnp.bfloat16).reshape(count, chans)

    def down_of(owner):
        return lax.dot_general(
            lax.dynamic_slice_in_dim(mixed, owner * own_rows, own_rows, 0),
            w_out,
            (((1,), (1,)), ((), ())),
            preferred_element_type=jnp.float32,
        )

    sent = swap(down_of(n_width - 1 - me).astype(jnp.bfloat16), "width")
    down = down_of(me) + sent.astype(jnp.float32)

    def mine(x):
        return lax.dynamic_slice_in_dim(x, me * own_rows, own_rows, 0)

    resid = (mine(features).astype(jnp.float32) + down).astype(jnp.bfloat16)
    wide = resid.astype(jnp.float32)
    sumsq = jnp.sum(wide * wide, -1)
    scores = jnp.dot(resid, heads, preferred_element_type=jnp.float32)
    norm = lax.rsqrt(sumsq / depth + 1e-06)
    scores = scores * norm[:, None]
    logits = scores[:, :-1]
    value = jnp.tanh(scores[:, -1])
    top = jnp.max(logits, -1, keepdims=True)
    lse = top[:, 0] + jnp.log(jnp.sum(jnp.exp(logits - top), -1))
    column = lax.broadcasted_iota(jnp.int32, logits.shape, 1)
    picked = jnp.sum(jnp.where(column == mine(interleave(moves).reshape(count, 1)), logits, 0.0), -1)
    target = jnp.broadcast_to(outcomes.astype(jnp.float32)[:, None], (games, block_len))
    position = here * block_len + lax.broadcasted_iota(jnp.int32, (games, block_len), 1)
    live = interleave(position < lengths[:, None]).reshape(count)
    loss = jnp.where(mine(live), lse - picked + (value - mine(target.reshape(count))) ** 2, 0.0)
    result = jnp.stack([loss, value])
    result = both(result, swap(result, "width"), "width", 1)
    result = result.reshape(2, games, block_len)
    return (restore(result[0]), restore(result[1]))


def solution(mesh):
    in_specs = (
        P("batch", "tm"),
        P("batch"),
        P("batch"),
        P("batch", "tm", "width"),
        P(None, ("tm", "batch"), "width"),
        P(None, "width"),
        P(None, "width"),
        P("width"),
        P(("tm", "batch"), "width"),
        P("width", None),
        P("width"),
    )
    out_specs = (P("batch", "tm"), P("batch", "tm"))
    return jax.shard_map(shards, mesh=mesh, in_specs=in_specs, out_specs=out_specs, check_vma=False)
```

time: 496 us -> 256 us (0.52)
  local copies, waits for them, and re-layouts: 133 us -> 4.02 us
  waiting for transfers between devices: 256 us -> 170 us
  other arithmetic: 48.4 us -> 8.2 us
  blocking collectives: 4.92 us -> 14 us
  Pallas kernels: 0 us -> 7.94 us
  matrix products: 21.2 us -> 27.3 us
    slice x56 -> x2, local copies, waits for them, and re-layouts: 97.9 us -> 0.09 us  [the longest x1 0.06 us: shards(): features.reshape(games, block_len // SUB, SUB, depth)]
    all_gather x3 -> x2, waiting for transfers between devices: 165 us -> 103 us  [the longest x1 95.6 us: shards(): w_full = lax.all_gather(w_branches, ('tm', 'batch'), axis=1, tiled=True)]
    ppermute x4 -> x5, waiting for transfers between devices: 5.49 us -> 65.8 us  [the longest x4 63.6 us: swap(): return lax.ppermute(value, axis, [(i, n - 1 - i) for i in range(n)])]
    reduce_scatter x1 -> x0, waiting for transfers between devices: 55.3 us -> none  [shards(): lax.psum_scatter(partial_down, 'width', scatter_dimension=1, tiled=True)]
    pad x28 -> x0, local copies, waits for them, and re-layouts: 29.4 us -> none  [shards(): summed, local = lax.associative_scan(link, (log_a, drive), axis=1)]
    psum x1 -> x0, waiting for transfers between devices: 28.3 us -> none  [shards(): lax.psum((local_logits, local_value, local_sq), 'width')]
    add x31 -> x1, other arithmetic: 23.7 us -> 0.01 us  [shards(): here * block_len + lax.broadcasted_iota(jnp.int32, (games, block_len), 1)]
    all_gather x0 -> x1, blocking collectives: none -> 14 us  [shards(): ends_all = lax.all_gather(ends, 'tm', axis=0)]
  transfers between devices with their start and end apart: 9 -> 7, of which waited for: 8 -> 6; matrix products, arithmetic and copies ran while one was open for 37% -> 11% of each run, Pallas kernels for 0% -> 3%
where the time goes in v1:
time: 256 us
  waiting for transfers between devices  170 us (66%)
  matrix products  27.3 us (11%)
  between operations  14.2 us (6%)
  blocking collectives  14 us (5%)
  starting transfers between devices  10.4 us (4%)
  other arithmetic  8.2 us (3%)
  Pallas kernels  7.94 us (3%)
  local copies, waits for them, and re-layouts  4.02 us (2%)
    all_gather x1, waiting for transfers between devices, shards(): w_full = lax.all_gather(w_branches, ('tm', 'batch'), axis=1, tiled=True)  95.6 us
    ppermute x4, waiting for transfers between devices, swap(): return lax.ppermute(value, axis, [(i, n - 1 - i) for i in range(n)])  63.6 us
    dot_general x1, matrix products, shards(): jnp.einsum('td,kdn->ktn', features, w_full, preferred_element_type=jnp.fl...  14.4 us
    all_gather x1, blocking collectives, shards(): ends_all = lax.all_gather(ends, 'tm', axis=0)  14 us
    dot_general x2, matrix products, down_of(): lax.dot_general(lax.dynamic_slice_in_dim(mixed, owner * own_rows, own_row...  8.83 us
    pallas_call x1, Pallas kernels, block_scan(): pl.pallas_call(scan_kernel, grid=(games, chans // cols), in_specs=[pl.Blo...  7.94 us
    all_gather x1, waiting for transfers between devices, shards(): w_out = lax.all_gather(w_down, ('tm', 'batch'), axis=0, tiled=True)  7 us
    ppermute x4, starting transfers between devices, swap(): return lax.ppermute(value, axis, [(i, n - 1 - i) for i in range(n)])  6.62 us
  transfers between devices with their start and end apart: 7, of which 6 were waited for; matrix products, arithmetic and copies ran while one was open for 11% of the time, Pallas kernels for 3%

profile of v1, /device:TPU:0, one launch (start us, length us, event | category | flops | bytes accessed | tf_op | source)
XLA Modules:
  0.0 256.0 jit_solution(16798479985064024625)
XLA Ops:
  7.2 0.7 all-gather.4.cloned.1.call-update
  7.9 0.7 all-gather.6.cloned.1.call-update
  8.6 1.8 copy.38
  10.5 3.1 %collective-permute-start = (bf16[512,1024]{1,0:T(8,128)(2,1)S(1)}, bf16[512,1024]{1,0:T(8,128)(2,1)}, u32[]{:S(2)}, u32[]{:S(2)}) collective-permute-start(bf16[512,1024]{1,0:T(8,128)(2,1)S(1)} %bitcast.75), channel_id=1, source_target_pairs={{0,1},{1,0},{2,3},{3,2},{4,5},{5,4},{6,7},{7,6},{8,9},{9,8},{10,11... | collective-permute-start | bytes 3145736 | tf_op jit(solution)/shard_map/ppermute | solution.py:16
  13.5 23.3 %collective-permute-done = bf16[512,1024]{1,0:T(8,128)(2,1)} collective-permute-done((bf16[512,1024]{1,0:T(8,128)(2,1)S(1)}, bf16[512,1024]{1,0:T(8,128)(2,1)}, u32[]{:S(2)}, u32[]{:S(2)}) %collective-permute-start) | collective-permute-done | bytes 1048608 | tf_op jit(solution)/shard_map/ppermute | solution.py:16
  36.8 1.4 broadcast_select_fusion.1
  38.2 0.2 pad_maximum_fusion
  38.4 3.7 %collective-permute-start.1 = (bf16[2,3,2048]{2,1,0:T(4,128)(2,1)S(1)}, bf16[2,3,2048]{2,1,0:T(4,128)(2,1)S(1)}, u32[]{:S(2)}, u32[]{:S(2)}) collective-permute-start(bf16[2,3,2048]{2,1,0:T(4,128)(2,1)S(1)} %bitcast.82), channel_id=1, source_target_pairs={{0,8},{8,16},{16,24},{1,9},{9,17},{17,25},{2,10},{10,18},{18,26},{... | collective-permute-start | bytes 73736 | tf_op jit(solution)/shard_map/ppermute | solution.py:21
  42.2 2.2 collective-permute-done.1
  44.4 95.6 %all-gather.4.cloned.1.call-done = bf16[4,2048,1024]{2,1,0:T(8,128)(2,1)} async-done(((bf16[4,128,1024]{2,1,0:T(8,128)(2,1)}), bf16[4,2048,1024]{2,1,0:T(8,128)(2,1)}) %all-gather.4.cloned.1.call-update) | async-done | bytes 16777232 | tf_op jit(solution)/shard_map/all_gather | solution.py:153
  140.0 3.5 %fusion.halo = f32[2,3,1024]{2,1,0:T(4,128)} fusion(bf16[2,3,2048]{2,1,0:T(4,128)(2,1)S(1)} %collective-permute-done.1, bf16[4,2048,1024]{2,1,0:T(8,128)(2,1)} %all-gather.4.cloned.1.call-done), kind=kOutput, calls=%fused_computation.1 | convolution fusion | flops 25165824 | bytes 4243456 | tf_op jit(solution)/shard_map/dot_general | solution.py:155
  143.5 14.4 %convolution_bitcast_fusion.proj = f32[4,512,1024]{2,1,0:T(8,128)} fusion(bf16[4,2048,1024]{2,1,0:T(8,128)(2,1)} %all-gather.4.cloned.1.call-done, bf16[512,1024]{1,0:T(8,128)(2,1)S(1)} %get-tuple-element.13, bf16[512,1024]{1,0:T(8,128)(2,1)S(1)} %get-tuple-element.12), kind=kOutput, calls=%fused_computation.2 | convolution fusion | flops 8594128896 | bytes 27262976 | tf_op jit(solution)/shard_map/td,kdn->ktn/dot_general | solution.py:154
  157.9 7.9 %shard_map.122 = (f32[512,1024]{1,0:T(8,128)}, f32[512,1024]{1,0:T(8,128)}, f32[2,2,1024]{2,1,0:T(2,128)}) custom-call(f32[4,512,1024]{2,1,0:T(8,128)} %convolution_bitcast_fusion.proj, f32[2,3,1024]{2,1,0:T(4,128)} %fusion.halo, f32[4,1024]{1,0:T(4,128)} %conv_w.1, f32[2,1024]{1,0:T(2,128)} %bias.1, f32[1,1024]{1,0:T(1,128)} %bitcast.86), custom_call_target="tpu_custom_call" | custom-call | flops 31457280 | bytes 12582912 | tf_op jit(solution)/shard_map/pallas_call | solution.py:97
  165.9 14.0 %all-gather = f32[8,2,1024]{2,1,0:T(2,128)S(1)} all-gather(f32[2,2,1024]{2,1,0:T(2,128)} %get-tuple-element.7), channel_id=2, replica_groups=mesh['tm'=4,'batch'=4,'width'=2] {'tm'}, dimensions={0}, use_global_device_ids=true | all-gather | bytes 81920 | tf_op jit(solution)/shard_map/all_gather | solution.py:160
  179.9 3.8 %fusion.2 = bf16[512,1024]{1,0:T(8,128)(2,1)} fusion(f32[512,1024]{1,0:T(8,128)} %get-tuple-element.5, f32[512,1024]{1,0:T(8,128)} %get-tuple-element.6, f32[2,1024]{1,0:T(2,128)S(1)} %fusion.24), kind=kLoop, calls=%fused_computation.9 | loop fusion | flops 1572864 | bytes 5251072 | tf_op jit(solution)/shard_map/convert_element_type | solution.py:166
  183.7 7.0 %all-gather.6.cloned.1.call-done = bf16[2048,1024]{1,0:T(8,128)(2,1)} async-done(((bf16[128,1024]{1,0:T(8,128)(2,1)}), bf16[2048,1024]{1,0:T(8,128)(2,1)}) %all-gather.6.cloned.1.call-update) | async-done | bytes 4194320 | tf_op jit(solution)/shard_map/all_gather | solution.py:159
  190.7 4.7 %convolution_convert_fusion = bf16[256,2048]{1,0:T(8,128)(2,1)} fusion(bf16[2048,1024]{1,0:T(8,128)(2,1)} %all-gather.6.cloned.1.call-done, bf16[512,1024]{1,0:T(8,128)(2,1)} %fusion.2, s32[]{:T(128)S(6)} %select_n.101), kind=kOutput, calls=%fused_computation.3 | convolution fusion | flops 1074266112 | bytes 5767172 | tf_op jit(solution)/shard_map/dot_general | solution.py:169
  195.4 1.5 collective-permute-start.2
  196.9 0.9 pad_maximum_fusion.1
  197.8 0.6 collective-permute-start.3
  198.5 0.1 reshape_reshape.8
  198.7 0.1 lt.26
  198.9 38.3 %collective-permute-done.3 = bf16[1024,363]{0,1:T(8,128)(2,1)} collective-permute-done((bf16[1024,363]{0,1:T(8,128)(2,1)}, bf16[1024,363]{0,1:T(8,128)(2,1)}, u32[]{:S(2)}, u32[]{:S(2)}) %collective-permute-start.3) | collective-permute-done | bytes 743456 | tf_op jit(solution)/shard_map/ppermute | solution.py:16
  237.2 1.5 broadcast_select_fusion.3
  238.7 4.2 %multiply_reduce_fusion = (f32[256]{0:T(256)S(1)}, bf16[256,2048]{1,0:T(8,128)(2,1)S(1)}) fusion(bf16[256,2048]{1,0:T(8,128)(2,1)} %collective-permute-done.2, bf16[2048,1024]{1,0:T(8,128)(2,1)} %all-gather.6.cloned.1.call-done, bf16[512,1024]{1,0:T(8,128)(2,1)S(1)} %copy-done.1, s32[]{:T(128)S(6)} %select_n.90, ...), kind=kOutput, calls=%fused_computation.11 | convolution fusion | flops 1079508736 | bytes 8914944 | tf_op jit(solution)/shard_map/dot_general | solution.py:169
  242.9 0.6 fusion.8
  243.6 0.1 exponential_reduce_fusion
  243.8 1.5 collective-permute-start.4
  245.3 2.1 collective-permute-done.4
  247.5 0.1 reshape_squeeze.6
  247.6 0.7 reshape.116
  248.4 0.7 reshape.117
  (38 shorter events, 1.0 us)
Async XLA Ops:
  7.2 132.8 %all-gather.4.cloned.1.call-start = ((), (), s32[]{:S(2)}) async-start(), calls=%async_computation | async-start | bytes 17825792 | tf_op jit(solution)/shard_map/all_gather | solution.py:153
  7.9 182.8 %all-gather.6.cloned.1.call-start = ((), (), s32[]{:S(2)}) async-start(), calls=%async_computation.1 | async-start | bytes 4456448 | tf_op jit(solution)/shard_map/all_gather | solution.py:159
  10.5 26.3 %collective-permute-start = (bf16[512,1024]{1,0:T(8,128)(2,1)S(1)}, bf16[512,1024]{1,0:T(8,128)(2,1)}, u32[]{:S(2)}, u32[]{:S(2)}) collective-permute-start(bf16[512,1024]{1,0:T(8,128)(2,1)S(1)} %bitcast.75), channel_id=1, source_target_pairs={{0,1},{1,0},{2,3},{3,2},{4,5},{5,4},{6,7},{7,6},{8,9},{9,8},{10,11... | collective-permute-start | bytes 3145736 | tf_op jit(solution)/shard_map/ppermute | solution.py:16
  38.1 4.0 %copy-start.2 = (bf16[1024]{0:T(1024)(128)(2,1)S(1)}, bf16[1024]{0:T(1024)(128)(2,1)}, u32[]{:S(2)}) copy-start(bf16[1024]{0:T(1024)(128)(2,1)} %param.21) | copy-start | bytes 6148
  38.4 5.9 %collective-permute-start.1 = (bf16[2,3,2048]{2,1,0:T(4,128)(2,1)S(1)}, bf16[2,3,2048]{2,1,0:T(4,128)(2,1)S(1)}, u32[]{:S(2)}, u32[]{:S(2)}) collective-permute-start(bf16[2,3,2048]{2,1,0:T(4,128)(2,1)S(1)} %bitcast.82), channel_id=1, source_target_pairs={{0,8},{8,16},{16,24},{1,9},{9,17},{17,25},{2,10},{10,18},{18,26},{... | collective-permute-start | bytes 73736 | tf_op jit(solution)/shard_map/ppermute | solution.py:21
  183.7 13.2 %copy-start = (bf16[1024,362]{0,1:T(8,128)(2,1)S(1)}, bf16[1024,362]{0,1:T(8,128)(2,1)}, u32[]{:S(2)}) copy-start(bf16[1024,362]{0,1:T(8,128)(2,1)} %param.20) | copy-start | bytes 2224132
  183.7 14.6 %copy-start.3 = (s32[2,256]{1,0:T(2,128)S(1)}, s32[2,256]{1,0:T(2,128)}, u32[]{:S(2)}) copy-start(s32[2,256]{1,0:T(2,128)} %param.11) | copy-start | bytes 6148
  183.7 14.9 %copy-start.4 = (s32[2]{0:T(128)S(1)}, s32[2]{0:T(128)}, u32[]{:S(2)}) copy-start(s32[2]{0:T(128)} %param.12) | copy-start | bytes 28
  183.7 15.1 %copy-start.5 = (s32[2]{0:T(128)S(1)}, s32[2]{0:T(128)}, u32[]{:S(2)}) copy-start(s32[2]{0:T(128)} %param.13) | copy-start | bytes 28
  195.4 43.3 %collective-permute-start.2 = (bf16[256,2048]{1,0:T(8,128)(2,1)}, bf16[256,2048]{1,0:T(8,128)(2,1)}, u32[]{:S(2)}, u32[]{:S(2)}) collective-permute-start(bf16[256,2048]{1,0:T(8,128)(2,1)} %convolution_convert_fusion), channel_id=1, source_target_pairs={{0,1},{1,0},{2,3},{3,2},{4,5},{5,4},{6,7},{7,6},{8,9},{9,8},{10,11... | collective-permute-start | bytes 3145736 | tf_op jit(solution)/shard_map/ppermute | solution.py:16
  197.8 39.4 %collective-permute-start.3 = (bf16[1024,363]{0,1:T(8,128)(2,1)}, bf16[1024,363]{0,1:T(8,128)(2,1)}, u32[]{:S(2)}, u32[]{:S(2)}) collective-permute-start(bf16[1024,363]{0,1:T(8,128)(2,1)} %pad_maximum_fusion.1), channel_id=1, source_target_pairs={{0,1},{1,0},{2,3},{3,2},{4,5},{5,4},{6,7},{7,6},{8,9},{9,8},{10,11... | collective-permute-start | bytes 2230280 | tf_op jit(solution)/shard_map/ppermute | solution.py:16
  198.9 39.8 %copy-start.1 = (bf16[512,1024]{1,0:T(8,128)(2,1)S(1)}, bf16[512,1024]{1,0:T(8,128)(2,1)}, u32[]{:S(2)}) copy-start(bf16[512,1024]{1,0:T(8,128)(2,1)} %fusion.2) | copy-start | bytes 3145732
  243.8 3.6 %collective-permute-start.4 = (f32[2,256]{1,0:T(2,128)S(1)}, f32[2,256]{1,0:T(2,128)S(1)}, u32[]{:S(2)}, u32[]{:S(2)}) collective-permute-start(f32[2,256]{1,0:T(2,128)S(1)} %pad_maximum_fusion.3), channel_id=1, source_target_pairs={{0,1},{1,0},{2,3},{3,2},{4,5},{5,4},{6,7},{7,6},{8,9},{9,8},{10,11... | collective-permute-start | bytes 6152 | tf_op jit(solution)/shard_map/ppermute | solution.py:16
Sparse Core Ops, SparseCore 0:
  10.2 129.7 all-gather.3
  142.2 48.5 all-gather.5

commit v2 on v1

v2 whole, which is shorter than its diff:
```python
import jax
import jax.numpy as jnp
from jax import lax
from jax.experimental import pallas as pl
from jax.experimental.pallas import tpu as pltpu
from jax.sharding import PartitionSpec as P

KERNEL = 4
SUB = 8
MESH = pl.DeviceIdType.MESH
STREAMS = tuple(range(6))


def swap(value, axis):
    n = lax.axis_size(axis)
    return lax.ppermute(value, axis, [(i, n - 1 - i) for i in range(n)])


def interleave(x):
    games, steps = x.shape[:2]
    return jnp.swapaxes(x.reshape(games, SUB, steps // SUB, *x.shape[2:]), 1, 2).reshape(x.shape)


def restore(x):
    games, steps = x.shape[:2]
    return jnp.swapaxes(x.reshape(games, steps // SUB, SUB, *x.shape[2:]), 1, 2).reshape(x.shape)


def both(own, other, axis, dim):
    first = lax.axis_index(axis) == 0
    return jnp.concatenate([jnp.where(first, own, other), jnp.where(first, other, own)], dim)


def core_kernel(
    emb, wb, wd, tail, conv_w, bias, rates,
    hg, pg, ends, wd_all, feat,
    w_all, acc, tails, halo, carry_s,
    loc, feat_s, feat_r, tail_s, tail_r, ring_s, ring_r, peer_s, peer_r,
):
    z, b, y = lax.axis_index("tm"), lax.axis_index("batch"), lax.axis_index("width")
    zn, bn, yn = lax.axis_size("tm"), lax.axis_size("batch"), lax.axis_size("width")
    x, core = b // 2, b % 2
    n = zn * (bn // 2)
    rows, chans = wd.shape
    count, half = emb.shape
    games = ends.shape[0]
    width_cut = chans // 2

    def spot(r):
        cx = r // zn
        cz = r % zn
        return cz + (cx % 2) * (zn - 1 - 2 * cz), cx

    r = x * zn + z + (x % 2) * (zn - 1 - 2 * z)

    def at(place, c=core, w=y):
        return {"tm": place[0], "batch": place[1] * 2 + c, "width": w}

    ahead, behind = at(spot((r + 1) % n)), at(spot((r + n - 1) % n))
    peer = at((z, x), 1 - core)
    partner = at((z, x), core, yn - 1 - y)
    later, earlier = ((z + 1) % zn, x), ((z + zn - 1) % zn, x)
    tail_to = [at(later), at(later, core, yn - 1 - y)]
    greet = [ahead, behind, peer, partner] + tail_to + [at(earlier), at(earlier, core, yn - 1 - y)]

    def first_row(chip):
        cz, cx = spot(chip)
        return (cz * bn + cx * 2) * rows

    own = first_row(r) + core * rows
    own = pl.multiple_of(own, rows)
    local = [
        pltpu.make_async_copy(wb, w_all.at[:, pl.ds(own, rows), :], loc.at[0]),
        pltpu.make_async_copy(wd, wd_all.at[pl.ds(own, rows), :], loc.at[1]),
        pltpu.make_async_copy(emb, feat.at[y], loc.at[2]),
        pltpu.make_async_copy(tail, tails.at[2], loc.at[3]),
    ]
    for copy in local:
        copy.start()
    barrier = pltpu.get_barrier_semaphore()
    for device in greet:
        pl.semaphore_signal(barrier, inc=1, device_id=device, device_id_type=MESH)
    pl.semaphore_wait(barrier, len(greet))
    for copy in local:
        copy.wait()

    def remote(src, dst, send, recv, device):
        return pltpu.make_async_remote_copy(
            src_ref=src, dst_ref=dst, send_sem=send, recv_sem=recv, device_id=device, device_id_type=MESH
        )

    def forward(s):
        return s in (0, 1, 4)

    def chip_of(s, t):
        return (r + n - t) % n if forward(s) else (r + t) % n

    def piece(s, chip, c):
        at_row = pl.ds(pl.multiple_of(first_row(chip) + c * rows, rows), rows)
        if s < 4:
            return w_all.at[s, at_row, :]
        return wd_all.at[at_row, pl.ds((s - 4) * width_cut, width_cut)]

    def hop(s, t):
        ref = piece(s, chip_of(s, t - 1), core)
        return remote(ref, ref, ring_s.at[s, t], ring_r.at[s, t], ahead if forward(s) else behind)

    def landed(s, t):
        ref = piece(s, chip_of(s, t), core)
        return remote(ref, ref, ring_s.at[s, t], ring_r.at[s, t], ahead if forward(s) else behind)

    def share(s, t):
        ref = piece(s, chip_of(s, t), core)
        return remote(ref, ref, peer_s.at[s, t], peer_r.at[s, t], peer)

    def shared(s, t):
        ref = piece(s, chip_of(s, t), 1 - core)
        return remote(ref, ref, peer_s.at[s, t], peer_r.at[s, t], peer)

    for s in STREAMS:
        hop(s, 1).start()
    swap_feat = remote(feat.at[y], feat.at[y], feat_s, feat_r, partner)
    swap_feat.start()
    tail_out = [
        remote(tails.at[2], tails.at[y], tail_s.at[i], tail_r.at[i], tail_to[i]) for i in range(2)
    ]
    for copy in tail_out:
        copy.start()
    for s in STREAMS:
        share(s, 0).start()
    acc[...] = jnp.zeros_like(acc)
    ref = feat.at[yn - 1 - y]
    remote(ref, ref, feat_s, feat_r, partner).wait_recv()

    tile = min(512, chans)
    eager = (2 * rows) % 128 == 0

    def product(s, start, depth):
        owner, col = start // half, pl.multiple_of(start % half, depth)
        left = feat[owner, :, pl.ds(col, depth)]

        @pl.loop(0, chans // tile)
        def _(j):
            cut = pl.ds(pl.multiple_of(j * tile, tile), tile)
            acc[s, :, cut] += jnp.dot(
                left,
                w_all[s, pl.ds(pl.multiple_of(start, depth), depth), cut],
                preferred_element_type=jnp.float32,
            )

    def compute(t):
        for s in STREAMS:
            shared(s, t).wait_recv()
            if s < 4 and eager:
                product(s, first_row(chip_of(s, t)), 2 * rows)

    @pl.loop(1, n)
    def _(t):
        for s in STREAMS:
            landed(s, t).wait_recv()

            @pl.when(t < n - 1)
            def _():
                hop(s, t + 1).start()

            share(s, t).start()
        compute(t - 1)

    compute(n - 1)
    if not eager:
        depth = min(256, half)

        @pl.loop(0, yn * half // depth)
        def _(i):
            for s in range(4):
                product(s, i * depth, depth)

    for i in range(2):
        ref = tails.at[y if i == 0 else yn - 1 - y]
        remote(ref, ref, tail_s.at[i], tail_r.at[i], tail_to[i]).wait_recv()
    cols = min(512, chans)
    blocks = chans // cols

    @pl.loop(0, blocks)
    def _(j):
        cut = pl.ds(pl.multiple_of(j * cols, cols), cols)
        edge = jnp.zeros((tails.shape[1], cols), jnp.float32)
        for owner in range(yn):
            edge += jnp.dot(
                tails[owner],
                w_all[1, owner * half : (owner + 1) * half, cut],
                preferred_element_type=jnp.float32,
            )
        halo[:, cut] = jnp.where(z > 0, edge, 0.0)

    steps = count // games
    seg = steps // SUB

    @pl.loop(0, games * blocks)
    def _(u):
        g, j = u // blocks, u % blocks
        cut = pl.ds(pl.multiple_of(j * cols, cols), cols)
        scan_block(
            acc, halo[pl.ds(pl.multiple_of(g * SUB, SUB), SUB), cut], conv_w[:, cut], bias[:, cut], rates[:, cut],
            hg, pg, ends, carry_s, g, cut, cols, seg,
        )

    for s in STREAMS:

        @pl.loop(1, n)
        def _(t):
            hop(s, t).wait_send()

        @pl.loop(0, n)
        def _(t):
            share(s, t).wait_send()

    swap_feat.wait_send()
    for copy in tail_out:
        copy.wait_send()


def scan_block(acc, halo, conv_w, bias, rates, hg, pg, ends, carry_s, g, cut, cols, seg):
    w = [conv_w[k : k + 1, :] for k in range(KERNEL)]
    b0, b1 = bias[0:1, :], bias[1:2, :]
    scale = -8.0 * rates
    row = lax.broadcasted_iota(jnp.int32, (SUB, cols), 0)

    def at(t):
        return pl.ds(pl.multiple_of((g * seg + t) * SUB, SUB), SUB)

    def before(j):
        rolled = pltpu.roll(acc[1, at(seg - j), cut], 1, 0)
        return jnp.where(row == 0, halo[KERNEL - 1 - j : KERNEL - j, :], rolled)

    def step(t, state):
        h, p, x1, x2, x3 = state
        here = at(t)
        x0 = acc[1, here, cut]
        conv = w[0] * x0 + w[1] * x1 + w[2] * x2 + w[3] * x3
        recur = jax.nn.sigmoid(acc[2, here, cut] + b0)
        inflow = jax.nn.sigmoid(acc[3, here, cut] + b1)
        a = jnp.exp(recur * scale)
        h = a * h + jnp.sqrt(1.0 - a * a) * inflow * conv
        p = a * p
        acc[0, here, cut] = jax.nn.gelu(acc[0, here, cut])
        acc[2, here, cut] = h
        acc[3, here, cut] = p
        return h, p, x0, x1, x2

    zero = jnp.zeros((SUB, cols), jnp.float32)
    h, p, _, _, _ = lax.fori_loop(
        0, seg, step, (zero, zero + 1.0, before(1), before(2), before(3)), unroll=4
    )
    run, dec = jnp.zeros((1, cols), jnp.float32), jnp.ones((1, cols), jnp.float32)
    for s in range(SUB):
        carry_s[0, s : s + 1, :] = run
        carry_s[1, s : s + 1, :] = dec
        run = p[s : s + 1] * run + h[s : s + 1]
        dec = p[s : s + 1] * dec
    ends[g, 0:1, cut] = run
    ends[g, 1:2, cut] = dec
    run, dec = carry_s[0], carry_s[1]

    def finish(t, _):
        here = at(t)
        gate, p = acc[0, here, cut], acc[3, here, cut]
        hg[here, cut] = (acc[2, here, cut] + p * run) * gate
        pg[here, cut] = p * dec * gate
        return 0

    lax.fori_loop(0, seg, finish, 0, unroll=4)


def core_block(emb, wb, wd, tail, conv_w, bias, rates, games):
    count, half = emb.shape
    rows, chans = wd.shape
    yn = lax.axis_size("width")
    n = lax.axis_size("tm") * (lax.axis_size("batch") // 2)
    depth = yn * half
    vmem = pl.BlockSpec(memory_space=pltpu.VMEM)
    hbm = pl.BlockSpec(memory_space=pl.ANY)
    dma = pltpu.SemaphoreType.DMA
    streams = len(STREAMS)
    return pl.pallas_call(
        core_kernel,
        in_specs=[hbm] * 4 + [vmem] * 3,
        out_specs=[vmem] * 5,
        out_shape=[
            jax.ShapeDtypeStruct((count, chans), jnp.float32),
            jax.ShapeDtypeStruct((count, chans), jnp.float32),
            jax.ShapeDtypeStruct((games, 2, chans), jnp.float32),
            jax.ShapeDtypeStruct((depth, chans), jnp.bfloat16),
            jax.ShapeDtypeStruct((yn, count, half), jnp.bfloat16),
        ],
        scratch_shapes=[
            pltpu.VMEM((4, depth, chans), jnp.bfloat16),
            pltpu.VMEM((4, count, chans), jnp.float32),
            pltpu.VMEM((3, games * SUB, half), jnp.bfloat16),
            pltpu.VMEM((games * SUB, chans), jnp.float32),
            pltpu.VMEM((2, SUB, min(512, chans)), jnp.float32),
            dma((4,)), dma, dma, dma((2,)), dma((2,)),
            dma((streams, n)), dma((streams, n)), dma((streams, n)), dma((streams, n)),
        ],
        compiler_params=pltpu.CompilerParams(
            collective_id=0, has_side_effects=True, vmem_limit_bytes=56 * 1024 * 1024
        ),
        cost_estimate=pl.CostEstimate(
            flops=8 * count * chans * depth, bytes_accessed=200_000_000, transcendentals=8 * count * chans
        ),
    )(emb, wb, wd, tail, conv_w, bias, rates.reshape(1, chans))


def shards(
    moves,
    lengths,
    outcomes,
    embedded,
    w_branches,
    conv_w,
    gate_bias,
    rates,
    w_down,
    w_policy,
    w_value,
):
    games, block_len, half = embedded.shape
    count = games * block_len
    chans = w_branches.shape[2]
    n_width = lax.axis_size("width")
    me = lax.axis_index("width")
    own_rows = count // n_width

    flat = interleave(embedded).reshape(count, half)
    heads = jnp.concatenate([w_policy, w_value[:, None]], 1)
    heads = both(heads, swap(heads, "width"), "width", 0)
    depth = n_width * half
    tail = flat.reshape(games, block_len // SUB, SUB, half)[:, 1 - KERNEL :, SUB - 1, :]
    tail = jnp.pad(tail, ((0, 0), (0, SUB + 1 - KERNEL), (0, 0))).reshape(games * SUB, half)
    hg, pg, ends, w_out, feat = core_block(
        flat, w_branches, w_down, tail, conv_w, gate_bias, rates, games
    )
    ends_all = lax.all_gather(ends, "tm", axis=0)
    state = jnp.zeros((games, chans), jnp.float32)
    here = lax.axis_index("tm")
    for j in range(lax.axis_size("tm") - 1):
        state = jnp.where(j < here, ends_all[j, :, 1] * state + ends_all[j, :, 0], state)
    mixed = hg.reshape(games, block_len, chans) + pg.reshape(games, block_len, chans) * state[:, None]
    mixed = mixed.astype(jnp.bfloat16).reshape(count, chans)

    def down_of(owner):
        return lax.dot_general(
            lax.dynamic_slice_in_dim(mixed, owner * own_rows, own_rows, 0),
            w_out,
            (((1,), (1,)), ((), ())),
            preferred_element_type=jnp.float32,
        )

    sent = swap(down_of(n_width - 1 - me).astype(jnp.bfloat16), "width")
    down = down_of(me) + sent.astype(jnp.float32)

    def mine(x):
        return lax.dynamic_slice_in_dim(x, me * own_rows, own_rows, 0)

    features = jnp.concatenate([mine(feat[i]) for i in range(n_width)], 1)
    resid = (features.astype(jnp.float32) + down).astype(jnp.bfloat16)
    wide = resid.astype(jnp.float32)
    sumsq = jnp.sum(wide * wide, -1)
    scores = jnp.dot(resid, heads, preferred_element_type=jnp.float32)
    norm = lax.rsqrt(sumsq / depth + 1e-06)
    scores = scores * norm[:, None]
    logits = scores[:, :-1]
    value = jnp.tanh(scores[:, -1])
    top = jnp.max(logits, -1, keepdims=True)
    lse = top[:, 0] + jnp.log(jnp.sum(jnp.exp(logits - top), -1))
    column = lax.broadcasted_iota(jnp.int32, logits.shape, 1)
    picked = jnp.sum(jnp.where(column == mine(interleave(moves).reshape(count, 1)), logits, 0.0), -1)
    target = jnp.broadcast_to(outcomes.astype(jnp.float32)[:, None], (games, block_len))
    position = here * block_len + lax.broadcasted_iota(jnp.int32, (games, block_len), 1)
    live = interleave(position < lengths[:, None]).reshape(count)
    loss = jnp.where(mine(live), lse - picked + (value - mine(target.reshape(count))) ** 2, 0.0)
    result = jnp.stack([loss, value])
    result = both(result, swap(result, "width"), "width", 1)
    result = result.reshape(2, games, block_len)
    return (restore(result[0]), restore(result[1]))


def solution(mesh):
    in_specs = (
        P("batch", "tm"),
        P("batch"),
        P("batch"),
        P("batch", "tm", "width"),
        P(None, ("tm", "batch"), "width"),
        P(None, "width"),
        P(None, "width"),
        P("width"),
        P(("tm", "batch"), "width"),
        P("width", None),
        P("width"),
    )
    out_specs = (P("batch", "tm"), P("batch", "tm"))
    return jax.shard_map(shards, mesh=mesh, in_specs=in_specs, out_specs=out_specs, check_vma=False)
```

time: 256 us -> 205 us (0.80)
  waiting for transfers between devices: 170 us -> 35.1 us
  Pallas kernels: 7.94 us -> 134 us
  matrix products: 27.3 us -> 5.86 us
  between operations: 14.2 us -> 0.88 us
  starting transfers between devices: 10.4 us -> 3.83 us
    pallas_call x1, Pallas kernels: 7.94 us -> 134 us  [core_block(): pl.pallas_call(core_kernel, in_specs=[hbm] * 4 + [vmem] * 3, out_specs=[v...]
    all_gather x2 -> x0, waiting for transfers between devices: 103 us -> none  [the longest x1 95.6 us: shards(): w_full = lax.all_gather(w_branches, ('tm', 'batch'), axis=1, tiled=True)]
    ppermute x4 -> x3, waiting for transfers between devices: 63.6 us -> 35.1 us  [swap(): return lax.ppermute(value, axis, [(i, n - 1 - i) for i in range(n)])]
    dot_general x2 -> x0, matrix products: 17.9 us -> none  [the longest x1 14.4 us: shards(): jnp.einsum('td,kdn->ktn', features, w_full, preferred_element_type=jnp.fl...]
    ppermute x1 -> x0, starting transfers between devices: 3.7 us -> none  [from_behind(): return lax.ppermute(value, axis, [(i, i + 1) for i in range(n - 1)])]
    dot_general x2, matrix products: 8.83 us -> 5.26 us  [down_of(): lax.dot_general(lax.dynamic_slice_in_dim(mixed, owner * own_rows, own_row...]
    ppermute x4 -> x3, starting transfers between devices: 6.62 us -> 3.83 us  [swap(): return lax.ppermute(value, axis, [(i, n - 1 - i) for i in range(n)])]
  transfers between devices with their start and end apart: 7 -> 3, of which waited for: 6 -> 2; matrix products, arithmetic and copies ran while one was open for 11% -> 2% of each run, Pallas kernels for 3% -> 0%
where the time goes in v2:
time: 205 us
  Pallas kernels  134 us (65%)
  waiting for transfers between devices  35.1 us (17%)
  blocking collectives  13.3 us (6%)
  local copies, waits for them, and re-layouts  6.52 us (3%)
  matrix products  5.86 us (3%)
  other arithmetic  5.74 us (3%)
  starting transfers between devices  3.83 us (2%)
    pallas_call x1, Pallas kernels, core_block(): pl.pallas_call(core_kernel, in_specs=[hbm] * 4 + [vmem] * 3, out_specs=[v...  134 us
    ppermute x3, waiting for transfers between devices, swap(): return lax.ppermute(value, axis, [(i, n - 1 - i) for i in range(n)])  35.1 us
    all_gather x1, blocking collectives, shards(): ends_all = lax.all_gather(ends, 'tm', axis=0)  13.3 us
    dot_general x2, matrix products, down_of(): lax.dot_general(lax.dynamic_slice_in_dim(mixed, owner * own_rows, own_row...  5.26 us
  transfers between devices with their start and end apart: 3, of which 2 were waited for; matrix products, arithmetic and copies ran while one was open for 2% of the time, Pallas kernels for 0%

profile of v2, /device:TPU:0, one launch (start us, length us, event | category | flops | bytes accessed | tf_op | source)
XLA Modules:
  0.0 205.0 jit_solution(4394188924193140182)
XLA Ops:
  0.6 1.4 copy.95
  2.1 0.6 pad_bitcast_fusion.tail
  2.7 1.6 copy.39
  4.3 133.7 %shard_map.122 = (f32[512,1024]{1,0:T(8,128)}, f32[512,1024]{1,0:T(8,128)}, f32[2,2,1024]{2,1,0:T(2,128)}, bf16[2048,1024]{1,0:T(8,128)(2,1)}, bf16[2,512,1024]{2,1,0:T(8,128)(2,1)}) custom-call(bf16[512,1024]{1,0:T(8,128)(2,1)} %bitcast.72, bf16[4,128,1024]{2,1,0:T(8,128)(2,1)} %wb.1, bf16[128,1024]{1,0:T(8,128)(2,1)} %wd.1, ...), custom_call_target="tpu_custom_call" | custom-call | flops 8589934592 | bytes 200000000 | tf_op jit(solution)/shard_map/pallas_call | solution.py:285
  138.0 13.3 %all-gather = f32[8,2,1024]{2,1,0:T(2,128)S(1)} all-gather(f32[2,2,1024]{2,1,0:T(2,128)} %get-tuple-element.10), channel_id=2, replica_groups=mesh['tm'=4,'batch'=4,'width'=2] {'tm'}, dimensions={0}, use_global_device_ids=true | all-gather | bytes 81920 | tf_op jit(solution)/shard_map/all_gather | solution.py:343
  151.4 2.9 %fusion.1 = bf16[512,1024]{1,0:T(8,128)(2,1)S(1)} fusion(f32[512,1024]{1,0:T(8,128)} %get-tuple-element.8, f32[512,1024]{1,0:T(8,128)} %get-tuple-element.9, f32[2,1024]{1,0:T(2,128)S(1)} %fusion.21), kind=kLoop, calls=%fused_computation.3 | loop fusion | flops 1572864 | bytes 5251072 | tf_op jit(solution)/shard_map/convert_element_type | solution.py:349
  154.3 0.5 copy-done.9
  154.8 2.3 %convolution_convert_fusion = bf16[256,2048]{1,0:T(8,128)(2,1)} fusion(bf16[2048,1024]{1,0:T(8,128)(2,1)S(1)} %copy-done.9, bf16[512,1024]{1,0:T(8,128)(2,1)S(1)} %fusion.1, s32[]{:T(128)S(6)} %select_n.87), kind=kOutput, calls=%fused_computation | convolution fusion | flops 1074266112 | bytes 5767172 | tf_op jit(solution)/shard_map/dot_general | solution.py:352
  157.2 1.5 collective-permute-start
  158.7 0.9 pad_maximum_fusion
  159.6 0.6 collective-permute-start.1
  160.2 0.1 reshape.112
  160.2 0.1 copy.45
  160.3 0.1 reshape_reshape.8
  160.4 0.1 broadcast_compare_fusion
  160.5 0.1 lt.27
  160.6 0.1 broadcast_bitcast_fusion
  160.7 0.2 fusion.29
  160.9 0.1 dynamic-slice_bitcast_fusion
  161.0 33.3 %collective-permute-done.1 = bf16[1024,363]{0,1:T(8,128)(2,1)} collective-permute-done((bf16[1024,363]{0,1:T(8,128)(2,1)}, bf16[1024,363]{0,1:T(8,128)(2,1)}, u32[]{:S(2)}, u32[]{:S(2)}) %collective-permute-start.1) | collective-permute-done | bytes 743456 | tf_op jit(solution)/shard_map/ppermute | solution.py:16
  194.3 1.5 broadcast_select_fusion.1
  195.8 2.9 %multiply_reduce_fusion = (f32[256]{0:T(256)S(1)}, bf16[256,2048]{1,0:T(8,128)(2,1)S(1)}) fusion(bf16[256,2048]{1,0:T(8,128)(2,1)} %collective-permute-done, bf16[2048,1024]{1,0:T(8,128)(2,1)S(1)} %copy-done.10, bf16[512,1024]{1,0:T(8,128)(2,1)S(1)} %copy-done.4, s32[]{:T(128)S(6)} %select_n.79, bf16[256,1024]{1,0:T(8,128)(2,1)S(1)} %get-tuple-element.32, ...), kind=kOutput, calls=%fused_computation.4 | convolution fusion | flops 1079508736 | bytes 7865348 | tf_op jit(solution)/shard_map/dot_general | solution.py:352
  198.7 0.6 fusion.6
  199.4 0.1 exponential_reduce_fusion
  199.5 0.1 dynamic-slice_select_fusion
  199.6 1.8 collective-permute-start.2
  201.4 1.8 collective-permute-done.2
  203.3 0.1 reshape_squeeze.6
  203.5 0.7 reshape.114
  204.1 0.1 reshape_squeeze.7
  204.2 0.1 copy.47
  204.3 0.7 reshape.115
  (37 shorter events, 0.3 us)
Async XLA Ops:
  0.6 2.1 %copy-start = (bf16[2,256,1024]{2,1,0:T(8,128)(2,1)S(1)}, bf16[2,256,1024]{2,1,0:T(8,128)(2,1)}, u32[]{:S(2)}) copy-start(bf16[2,256,1024]{2,1,0:T(8,128)(2,1)} %param.14) | copy-start | bytes 3145732
  151.4 3.5 %copy-start.9 = (bf16[2048,1024]{1,0:T(8,128)(2,1)S(1)}, bf16[2048,1024]{1,0:T(8,128)(2,1)}, u32[]{:S(2)}) copy-start(bf16[2048,1024]{1,0:T(8,128)(2,1)} %get-tuple-element.11) | copy-start | bytes 12582916
  154.3 2.9 %copy-start.3 = (bf16[512,1024]{1,0:T(8,128)(2,1)}, bf16[512,1024]{1,0:T(8,128)(2,1)S(1)}, u32[]{:S(2)}) copy-start(bf16[512,1024]{1,0:T(8,128)(2,1)S(1)} %fusion.1) | copy-start | bytes 3145732
  154.8 3.8 %copy-start.5 = (bf16[1024]{0:T(1024)(128)(2,1)S(1)}, bf16[1024]{0:T(1024)(128)(2,1)}, u32[]{:S(2)}) copy-start(bf16[1024]{0:T(1024)(128)(2,1)} %param.21) | copy-start | bytes 6148
  154.8 3.8 %copy-start.1 = (bf16[1024,362]{0,1:T(8,128)(2,1)S(1)}, bf16[1024,362]{0,1:T(8,128)(2,1)}, u32[]{:S(2)}) copy-start(bf16[1024,362]{0,1:T(8,128)(2,1)} %param.20) | copy-start | bytes 2224132
  154.8 5.3 %copy-start.6 = (s32[2,256]{1,0:T(2,128)S(1)}, s32[2,256]{1,0:T(2,128)}, u32[]{:S(2)}) copy-start(s32[2,256]{1,0:T(2,128)} %param.11) | copy-start | bytes 6148
  154.8 5.6 %copy-start.7 = (s32[2]{0:T(128)S(1)}, s32[2]{0:T(128)}, u32[]{:S(2)}) copy-start(s32[2]{0:T(128)} %param.12) | copy-start | bytes 28
  154.8 5.8 %copy-start.8 = (s32[2]{0:T(128)S(1)}, s32[2]{0:T(128)}, u32[]{:S(2)}) copy-start(s32[2]{0:T(128)} %param.13) | copy-start | bytes 28
  154.8 5.9 %copy-start.2 = (bf16[2,512,1024]{2,1,0:T(8,128)(2,1)S(1)}, bf16[2,512,1024]{2,1,0:T(8,128)(2,1)}, u32[]{:S(2)}) copy-start(bf16[2,512,1024]{2,1,0:T(8,128)(2,1)} %get-tuple-element.7) | copy-start | bytes 6291460
  157.2 38.6 %collective-permute-start = (bf16[256,2048]{1,0:T(8,128)(2,1)}, bf16[256,2048]{1,0:T(8,128)(2,1)}, u32[]{:S(2)}, u32[]{:S(2)}) collective-permute-start(bf16[256,2048]{1,0:T(8,128)(2,1)} %convolution_convert_fusion), channel_id=1, source_target_pairs={{0,1},{1,0},{2,3},{3,2},{4,5},{5,4},{6,7},{7,6},{8,9},{9,8},{10,11... | collective-permute-start | bytes 3145736 | tf_op jit(solution)/shard_map/ppermute | solution.py:16
  159.6 34.7 %collective-permute-start.1 = (bf16[1024,363]{0,1:T(8,128)(2,1)}, bf16[1024,363]{0,1:T(8,128)(2,1)}, u32[]{:S(2)}, u32[]{:S(2)}) collective-permute-start(bf16[1024,363]{0,1:T(8,128)(2,1)} %pad_maximum_fusion), channel_id=1, source_target_pairs={{0,1},{1,0},{2,3},{3,2},{4,5},{5,4},{6,7},{7,6},{8,9},{9,8},{10,11... | collective-permute-start | bytes 2230280 | tf_op jit(solution)/shard_map/ppermute | solution.py:16
  160.7 35.1 %copy-start.10 = (bf16[2048,1024]{1,0:T(8,128)(2,1)S(1)}, bf16[2048,1024]{1,0:T(8,128)(2,1)}, u32[]{:S(2)}) copy-start(bf16[2048,1024]{1,0:T(8,128)(2,1)} %get-tuple-element.11) | copy-start | bytes 12582916
  160.9 34.9 %copy-start.4 = (bf16[512,1024]{1,0:T(8,128)(2,1)S(1)}, bf16[512,1024]{1,0:T(8,128)(2,1)}, u32[]{:S(2)}) copy-start(bf16[512,1024]{1,0:T(8,128)(2,1)} %copy-done.3) | copy-start | bytes 3145732
  199.6 3.6 %collective-permute-start.2 = (f32[2,256]{1,0:T(2,128)S(1)}, f32[2,256]{1,0:T(2,128)S(1)}, u32[]{:S(2)}, u32[]{:S(2)}) collective-permute-start(f32[2,256]{1,0:T(2,128)S(1)} %pad_maximum_fusion.2), channel_id=1, source_target_pairs={{0,1},{1,0},{2,3},{3,2},{4,5},{5,4},{6,7},{7,6},{8,9},{9,8},{10,11... | collective-permute-start | bytes 6152 | tf_op jit(solution)/shard_map/ppermute | solution.py:16

commit v3 on v2

--- a/solution.py
+++ b/solution.py
@@ -33,9 +33,9 @@
 
 def core_kernel(
     emb, wb, wd, tail, conv_w, bias, rates,
-    hg, pg, ends, wd_all, feat,
-    w_all, acc, tails, halo, carry_s,
-    loc, feat_s, feat_r, tail_s, tail_r, ring_s, ring_r, peer_s, peer_r,
+    resid,
+    w_all, acc, tails, halo, carry_s, wd_all, feat, ends, state, mixed, out_buf, in_buf, kept,
+    loc, feat_s, feat_r, tail_s, tail_r, ring_s, ring_r, peer_s, peer_r, ends_s, ends_r, out_s, out_r,
 ):
     z, b, y = lax.axis_index("tm"), lax.axis_index("batch"), lax.axis_index("width")
     zn, bn, yn = lax.axis_size("tm"), lax.axis_size("batch"), lax.axis_size("width")
@@ -43,7 +43,7 @@
     n = zn * (bn // 2)
     rows, chans = wd.shape
     count, half = emb.shape
-    games = ends.shape[0]
+    games = ends.shape[1]
     width_cut = chans // 2
 
     def spot(r):
@@ -62,6 +62,7 @@
     later, earlier = ((z + 1) % zn, x), ((z + zn - 1) % zn, x)
     tail_to = [at(later), at(later, core, yn - 1 - y)]
     greet = [ahead, behind, peer, partner] + tail_to + [at(earlier), at(earlier, core, yn - 1 - y)]
+    greet += [at(((z + d) % zn, x)) for d in range(2, zn - 1)]
 
     def first_row(chip):
         cz, cx = spot(chip)
@@ -202,8 +203,63 @@
         cut = pl.ds(pl.multiple_of(j * cols, cols), cols)
         scan_block(
             acc, halo[pl.ds(pl.multiple_of(g * SUB, SUB), SUB), cut], conv_w[:, cut], bias[:, cut], rates[:, cut],
-            hg, pg, ends, carry_s, g, cut, cols, seg,
+            ends, carry_s, z, g, cut, cols, seg,
         )
+
+    def relay(d, source):
+        ref = ends.at[source]
+        return remote(ref, ref, ends_s.at[d], ends_r.at[d], at(((z + d) % zn, x)))
+
+    for d in range(1, zn):
+        relay(d, z).start()
+    for d in range(1, zn):
+        relay(d, (z + zn - d) % zn).wait_recv()
+    for g in range(games):
+        run = jnp.zeros((1, chans), jnp.float32)
+        for j in range(zn - 1):
+            run = jnp.where(j < z, ends[j, g, 1:2, :] * run + ends[j, g, 0:1, :], run)
+        state[g : g + 1, :] = run
+    for g in range(games):
+        run = state[g : g + 1, :]
+
+        @pl.loop(0, steps // 16)
+        def _(i):
+            here = pl.ds(pl.multiple_of(g * steps + i * 16, 16), 16)
+            mixed[here, :] = (acc[2, here, :] + acc[3, here, :] * run).astype(jnp.bfloat16)
+
+    parts, own_rows, part = out_buf.shape
+    mine = pl.ds(pl.multiple_of(y * own_rows, own_rows), own_rows)
+    theirs = pl.ds(pl.multiple_of((yn - 1 - y) * own_rows, own_rows), own_rows)
+
+    def down(which, j):
+        return lax.dot_general(
+            mixed[which, :],
+            wd_all[j * part : (j + 1) * part, :],
+            (((1,), (1,)), ((), ())),
+            preferred_element_type=jnp.float32,
+        )
+
+    def exchange(j):
+        return remote(out_buf.at[j], in_buf.at[j], out_s.at[j], out_r.at[j], partner)
+
+    for j in range(parts):
+        out_buf[j] = down(theirs, j).astype(jnp.bfloat16)
+        if j:
+            exchange(j - 1).start()
+    kept[0] = down(mine, 0)
+    exchange(parts - 1).start()
+    for j in range(1, parts):
+        kept[j] = down(mine, j)
+    for j in range(parts):
+        exchange(j).wait_recv()
+        first = j * part
+        base = feat[first // half, mine, first % half : first % half + part].astype(jnp.float32)
+        total = kept[j] + in_buf[j].astype(jnp.float32)
+        resid[:, first : first + part] = (base + total).astype(jnp.bfloat16)
+    for j in range(parts):
+        exchange(j).wait_send()
+    for d in range(1, zn):
+        relay(d, z).wait_send()
 
     for s in STREAMS:
 
@@ -220,7 +276,7 @@
         copy.wait_send()
 
 
-def scan_block(acc, halo, conv_w, bias, rates, hg, pg, ends, carry_s, g, cut, cols, seg):
+def scan_block(acc, halo, conv_w, bias, rates, ends, carry_s, z, g, cut, cols, seg):
     w = [conv_w[k : k + 1, :] for k in range(KERNEL)]
     b0, b1 = bias[0:1, :], bias[1:2, :]
     scale = -8.0 * rates
@@ -258,15 +314,15 @@
         carry_s[1, s : s + 1, :] = dec
         run = p[s : s + 1] * run + h[s : s + 1]
         dec = p[s : s + 1] * dec
-    ends[g, 0:1, cut] = run
-    ends[g, 1:2, cut] = dec
+    ends[z, g, 0:1, cut] = run
+    ends[z, g, 1:2, cut] = dec
     run, dec = carry_s[0], carry_s[1]
 
     def finish(t, _):
         here = at(t)
         gate, p = acc[0, here, cut], acc[3, here, cut]
-        hg[here, cut] = (acc[2, here, cut] + p * run) * gate
-        pg[here, cut] = p * dec * gate
+        acc[2, here, cut] = (acc[2, here, cut] + p * run) * gate
+        acc[3, here, cut] = p * dec * gate
         return 0
 
     lax.fori_loop(0, seg, finish, 0, unroll=4)
@@ -282,25 +338,32 @@
     hbm = pl.BlockSpec(memory_space=pl.ANY)
     dma = pltpu.SemaphoreType.DMA
     streams = len(STREAMS)
+    zn = lax.axis_size("tm")
+    own_rows = count // yn
+    part = min(512, half)
+    parts = depth // part
     return pl.pallas_call(
         core_kernel,
         in_specs=[hbm] * 4 + [vmem] * 3,
-        out_specs=[vmem] * 5,
-        out_shape=[
-            jax.ShapeDtypeStruct((count, chans), jnp.float32),
-            jax.ShapeDtypeStruct((count, chans), jnp.float32),
-            jax.ShapeDtypeStruct((games, 2, chans), jnp.float32),
-            jax.ShapeDtypeStruct((depth, chans), jnp.bfloat16),
-            jax.ShapeDtypeStruct((yn, count, half), jnp.bfloat16),
-        ],
+        out_specs=vmem,
+        out_shape=jax.ShapeDtypeStruct((own_rows, depth), jnp.bfloat16),
         scratch_shapes=[
             pltpu.VMEM((4, depth, chans), jnp.bfloat16),
             pltpu.VMEM((4, count, chans), jnp.float32),
             pltpu.VMEM((3, games * SUB, half), jnp.bfloat16),
             pltpu.VMEM((games * SUB, chans), jnp.float32),
             pltpu.VMEM((2, SUB, min(512, chans)), jnp.float32),
+            pltpu.VMEM((depth, chans), jnp.bfloat16),
+            pltpu.VMEM((yn, count, half), jnp.bfloat16),
+            pltpu.VMEM((zn, games, 2, chans), jnp.float32),
+            pltpu.VMEM((games, chans), jnp.float32),
+            pltpu.VMEM((count, chans), jnp.bfloat16),
+            pltpu.VMEM((parts, own_rows, part), jnp.bfloat16),
+            pltpu.VMEM((parts, own_rows, part), jnp.bfloat16),
+            pltpu.VMEM((parts, own_rows, part), jnp.float32),
             dma((4,)), dma, dma, dma((2,)), dma((2,)),
             dma((streams, n)), dma((streams, n)), dma((streams, n)), dma((streams, n)),
+            dma((zn,)), dma((zn,)), dma((parts,)), dma((parts,)),
         ],
         compiler_params=pltpu.CompilerParams(
             collective_id=0, has_side_effects=True, vmem_limit_bytes=56 * 1024 * 1024
@@ -326,7 +389,6 @@
 ):
     games, block_len, half = embedded.shape
     count = games * block_len
-    chans = w_branches.shape[2]
     n_width = lax.axis_size("width")
     me = lax.axis_index("width")
     own_rows = count // n_width
@@ -337,33 +399,12 @@
     depth = n_width * half
     tail = flat.reshape(games, block_len // SUB, SUB, half)[:, 1 - KERNEL :, SUB - 1, :]
     tail = jnp.pad(tail, ((0, 0), (0, SUB + 1 - KERNEL), (0, 0))).reshape(games * SUB, half)
-    hg, pg, ends, w_out, feat = core_block(
-        flat, w_branches, w_down, tail, conv_w, gate_bias, rates, games
-    )
-    ends_all = lax.all_gather(ends, "tm", axis=0)
-    state = jnp.zeros((games, chans), jnp.float32)
+    resid = core_block(flat, w_branches, w_down, tail, conv_w, gate_bias, rates, games)
     here = lax.axis_index("tm")
-    for j in range(lax.axis_size("tm") - 1):
-        state = jnp.where(j < here, ends_all[j, :, 1] * state + ends_all[j, :, 0], state)
-    mixed = hg.reshape(games, block_len, chans) + pg.reshape(games, block_len, chans) * state[:, None]
-    mixed = mixed.astype(jnp.bfloat16).reshape(count, chans)
-
-    def down_of(owner):
-        return lax.dot_general(
-            lax.dynamic_slice_in_dim(mixed, owner * own_rows, own_rows, 0),
-            w_out,
-            (((1,), (1,)), ((), ())),
-            preferred_element_type=jnp.float32,
-        )
-
-    sent = swap(down_of(n_width - 1 - me).astype(jnp.bfloat16), "width")
-    down = down_of(me) + sent.astype(jnp.float32)
 
     def mine(x):
         return lax.dynamic_slice_in_dim(x, me * own_rows, own_rows, 0)
 
-    features = jnp.concatenate([mine(feat[i]) for i in range(n_width)], 1)
-    resid = (features.astype(jnp.float32) + down).astype(jnp.bfloat16)
     wide = resid.astype(jnp.float32)
     sumsq = jnp.sum(wide * wide, -1)
     scores = jnp.dot(resid, heads, preferred_element_type=jnp.float32)

time: 205 us -> 185 us (0.902)
  Pallas kernels: 134 us -> 167 us
  waiting for transfers between devices: 35.1 us -> 3.08 us
  blocking collectives: 13.3 us -> 0 us
  matrix products: 5.86 us -> 0.59 us
  other arithmetic: 5.74 us -> 3.47 us
    pallas_call x1, Pallas kernels: 134 us -> 167 us  [core_block(): pl.pallas_call(core_kernel, in_specs=[hbm] * 4 + [vmem] * 3, out_specs=vm...]
    ppermute x3 -> x2, waiting for transfers between devices: 35.1 us -> 3.08 us  [swap(): return lax.ppermute(value, axis, [(i, n - 1 - i) for i in range(n)])]
    all_gather x1 -> x0, blocking collectives: 13.3 us -> none  [shards(): ends_all = lax.all_gather(ends, 'tm', axis=0)]
    dot_general x2 -> x0, matrix products: 5.26 us -> none  [down_of(): lax.dot_general(lax.dynamic_slice_in_dim(mixed, owner * own_rows, own_row...]
    convert_element_type x1 -> x0, other arithmetic: 2.9 us -> none  [shards(): mixed = mixed.astype(jnp.bfloat16).reshape(count, chans)]
  transfers between devices with their start and end apart: 3 -> 2, of which waited for: 2 -> 1; matrix products, arithmetic and copies ran while one was open for 2% -> 2% of each run, Pallas kernels for 0% -> 91%
where the time goes in v3:
time: 185 us
  Pallas kernels  167 us (90%)
  local copies, waits for them, and re-layouts  5.97 us (3%)
  starting transfers between devices  3.63 us (2%)
  other arithmetic  3.47 us (2%)
  waiting for transfers between devices  3.08 us (2%)
    pallas_call x1, Pallas kernels, core_block(): pl.pallas_call(core_kernel, in_specs=[hbm] * 4 + [vmem] * 3, out_specs=vm...  167 us
  transfers between devices with their start and end apart: 2, of which 1 were waited for; matrix products, arithmetic and copies ran while one was open for 2% of the time, Pallas kernels for 91%

profile of v3, /device:TPU:0, one launch (start us, length us, event | category | flops | bytes accessed | tf_op | source)
XLA Modules:
  0.0 184.5 jit_solution(6886920763970002270)
XLA Ops:
  0.6 0.0 copy-start
  0.6 0.8 broadcast_in_dim.20
  1.4 1.2 pad_maximum_fusion
  2.6 3.1 %collective-permute-start = (bf16[1024,363]{0,1:T(8,128)(2,1)S(1)}, bf16[1024,363]{0,1:T(8,128)(2,1)S(1)}, u32[]{:S(2)}, u32[]{:S(2)}) collective-permute-start(bf16[1024,363]{0,1:T(8,128)(2,1)S(1)} %pad_maximum_fusion), channel_id=1, source_target_pairs={{0,1},{1,0},{2,3},{3,2},{4,5},{5,4},{6,7},{7,6},{8,9},{9,8},{10,11... | collective-permute-start | bytes 2230280 | tf_op jit(solution)/shard_map/ppermute | solution.py:16
  5.7 1.6 copy.19
  7.2 0.1 copy.26
  7.3 0.6 pad_bitcast_fusion.tail
  8.0 0.0 copy-start.3
  8.0 167.0 %shard_map.122 = bf16[256,2048]{1,0:T(8,128)(2,1)} custom-call(bf16[512,1024]{1,0:T(8,128)(2,1)} %bitcast.27, bf16[4,128,1024]{2,1,0:T(8,128)(2,1)} %wb.1, bf16[128,1024]{1,0:T(8,128)(2,1)} %wd.1, bf16[16,1024]{1,0:T(8,128)(2,1)} %pad_bitcast_fusion.tail, f32[4,1024]{1,0:T(4,128)} %conv_w.1, f32[2,1024]{1,0:T(2,128)} %bias.1, f32[1,1024]{1,0:T(1,128)} %bitcast.36), custom_call_target="tpu_custom_call" | custom-call | flops 8589934592 | bytes 200000000 | tf_op jit(solution)/shard_map/pallas_call | solution.py:345
  175.0 0.0 copy-start.1
  175.0 0.1 broadcast_compare_fusion
  175.1 0.1 lt.21
  175.2 0.1 broadcast_bitcast_fusion
  175.3 0.1 reshape.67
  175.3 0.1 copy.20
  175.4 0.1 reshape_reshape.8
  175.5 1.5 multiply_reduce_fusion
  177.1 0.0 collective-permute-done
  177.1 0.4 broadcast_select_fusion.1
  177.5 0.8 copy-done.2
  178.3 0.6 fusion.4
  178.9 0.1 slice_reduce_fusion
  179.0 0.1 exponential_reduce_fusion
  179.1 0.1 dynamic-slice_select_fusion
  179.2 0.6 collective-permute-start.1
  179.7 3.1 %collective-permute-done.1 = f32[2,256]{1,0:T(2,128)S(1)} collective-permute-done((f32[2,256]{1,0:T(2,128)S(1)}, f32[2,256]{1,0:T(2,128)S(1)}, u32[]{:S(2)}, u32[]{:S(2)}) %collective-permute-start.1) | collective-permute-done | bytes 2080 | tf_op jit(solution)/shard_map/ppermute | solution.py:16
  182.9 0.1 reshape_squeeze.6
  183.0 0.1 copy.21
  183.0 0.7 reshape.69
  183.7 0.1 reshape_squeeze.7
  183.8 0.1 copy.22
  183.8 0.7 reshape.70
  (18 shorter events, 0.1 us)
Async XLA Ops:
  0.6 5.0 %copy-start = (bf16[2,256,1024]{2,1,0:T(8,128)(2,1)S(1)}, bf16[2,256,1024]{2,1,0:T(8,128)(2,1)}, u32[]{:S(2)}) copy-start(bf16[2,256,1024]{2,1,0:T(8,128)(2,1)} %param.14) | copy-start | bytes 3145732
  2.6 174.5 %collective-permute-start = (bf16[1024,363]{0,1:T(8,128)(2,1)S(1)}, bf16[1024,363]{0,1:T(8,128)(2,1)S(1)}, u32[]{:S(2)}, u32[]{:S(2)}) collective-permute-start(bf16[1024,363]{0,1:T(8,128)(2,1)S(1)} %pad_maximum_fusion), channel_id=1, source_target_pairs={{0,1},{1,0},{2,3},{3,2},{4,5},{5,4},{6,7},{7,6},{8,9},{9,8},{10,11... | collective-permute-start | bytes 2230280 | tf_op jit(solution)/shard_map/ppermute | solution.py:16
  8.0 167.0 %copy-start.4 = (s32[2]{0:T(128)S(1)}, s32[2]{0:T(128)}, u32[]{:S(2)}) copy-start(s32[2]{0:T(128)} %param.12) | copy-start | bytes 28
  8.0 167.2 %copy-start.5 = (s32[2]{0:T(128)S(1)}, s32[2]{0:T(128)}, u32[]{:S(2)}) copy-start(s32[2]{0:T(128)} %param.13) | copy-start | bytes 28
  8.0 167.3 %copy-start.3 = (s32[2,256]{1,0:T(2,128)S(1)}, s32[2,256]{1,0:T(2,128)}, u32[]{:S(2)}) copy-start(s32[2,256]{1,0:T(2,128)} %param.11) | copy-start | bytes 6148
  175.0 2.1 %copy-start.1 = (bf16[1024,362]{0,1:T(8,128)(2,1)S(1)}, bf16[1024,362]{0,1:T(8,128)(2,1)}, u32[]{:S(2)}) copy-start(bf16[1024,362]{0,1:T(8,128)(2,1)} %param.20) | copy-start | bytes 2224132
  177.1 1.2 copy-start.2
  179.2 3.6 %collective-permute-start.1 = (f32[2,256]{1,0:T(2,128)S(1)}, f32[2,256]{1,0:T(2,128)S(1)}, u32[]{:S(2)}, u32[]{:S(2)}) collective-permute-start(f32[2,256]{1,0:T(2,128)S(1)} %pad_maximum_fusion.2), channel_id=1, source_target_pairs={{0,1},{1,0},{2,3},{3,2},{4,5},{5,4},{6,7},{7,6},{8,9},{9,8},{10,11... | collective-permute-start | bytes 6152 | tf_op jit(solution)/shard_map/ppermute | solution.py:16

commit v4 on v3

--- a/solution.py
+++ b/solution.py
@@ -9,6 +9,7 @@
 SUB = 8
 MESH = pl.DeviceIdType.MESH
 STREAMS = tuple(range(6))
+LAG = 2
 
 
 def swap(value, axis):
@@ -118,7 +119,7 @@
         ref = piece(s, chip_of(s, t), 1 - core)
         return remote(ref, ref, peer_s.at[s, t], peer_r.at[s, t], peer)
 
-    for s in STREAMS:
+    for s in STREAMS[:4]:
         hop(s, 1).start()
     swap_feat = remote(feat.at[y], feat.at[y], feat_s, feat_r, partner)
     swap_feat.start()
@@ -150,21 +151,34 @@
             )
 
     def compute(t):
-        for s in STREAMS:
+        for s in STREAMS[:4]:
             shared(s, t).wait_recv()
-            if s < 4 and eager:
+            if eager:
                 product(s, first_row(chip_of(s, t)), 2 * rows)
+
+    def pump(s, t):
+        landed(s, t).wait_recv()
+
+        @pl.when(t < n - 1)
+        def _():
+            hop(s, t + 1).start()
+
+        share(s, t).start()
 
     @pl.loop(1, n)
     def _(t):
-        for s in STREAMS:
-            landed(s, t).wait_recv()
-
-            @pl.when(t < n - 1)
+        for s in STREAMS[:4]:
+            pump(s, t)
+        for s in STREAMS[4:]:
+
+            @pl.when(t == LAG)
             def _():
-                hop(s, t + 1).start()
-
-            share(s, t).start()
+                hop(s, 1).start()
+
+            @pl.when(t > LAG)
+            def _():
+                pump(s, t - LAG)
+
         compute(t - 1)
 
     compute(n - 1)
@@ -200,6 +214,16 @@
     @pl.loop(0, games * blocks)
     def _(u):
         g, j = u // blocks, u % blocks
+        for s in STREAMS[4:]:
+
+            @pl.when(u == 0)
+            def _():
+                pump(s, n - 2)
+
+            @pl.when(u == games * blocks - 1)
+            def _():
+                pump(s, n - 1)
+
         cut = pl.ds(pl.multiple_of(j * cols, cols), cols)
         scan_block(
             acc, halo[pl.ds(pl.multiple_of(g * SUB, SUB), SUB), cut], conv_w[:, cut], bias[:, cut], rates[:, cut],
@@ -226,6 +250,12 @@
         def _(i):
             here = pl.ds(pl.multiple_of(g * steps + i * 16, 16), 16)
             mixed[here, :] = (acc[2, here, :] + acc[3, here, :] * run).astype(jnp.bfloat16)
+
+    for s in STREAMS[4:]:
+
+        @pl.loop(0, n)
+        def _(t):
+            shared(s, t).wait_recv()
 
     parts, own_rows, part = out_buf.shape
     mine = pl.ds(pl.multiple_of(y * own_rows, own_rows), own_rows)

time: 185 us -> 181 us (0.978)
  Pallas kernels: 167 us -> 164 us
    pallas_call x1, Pallas kernels: 167 us -> 164 us  [core_block(): pl.pallas_call(core_kernel, in_specs=[hbm] * 4 + [vmem] * 3, out_specs=vm...]
  transfers between devices with their start and end apart: 2 -> 2, of which waited for: 1 -> 1; matrix products, arithmetic and copies ran while one was open for 2% -> 2% of each run, Pallas kernels for 91% -> 90%
where the time goes in v4:
time: 181 us
  Pallas kernels  164 us (91%)
  local copies, waits for them, and re-layouts  5.97 us (3%)
  starting transfers between devices  3.61 us (2%)
  other arithmetic  3.47 us (2%)
  waiting for transfers between devices  3.1 us (2%)
    pallas_call x1, Pallas kernels, core_block(): pl.pallas_call(core_kernel, in_specs=[hbm] * 4 + [vmem] * 3, out_specs=vm...  164 us
  transfers between devices with their start and end apart: 2, of which 1 were waited for; matrix products, arithmetic and copies ran while one was open for 2% of the time, Pallas kernels for 90%

profile of v4, /device:TPU:0, one launch (start us, length us, event | category | flops | bytes accessed | tf_op | source)
XLA Modules:
  0.0 181.1 jit_solution(15521215281451857437)
XLA Ops:
  0.6 0.8 broadcast_in_dim.20
  1.4 1.2 pad_maximum_fusion
  2.6 3.1 %collective-permute-start = (bf16[1024,363]{0,1:T(8,128)(2,1)S(1)}, bf16[1024,363]{0,1:T(8,128)(2,1)S(1)}, u32[]{:S(2)}, u32[]{:S(2)}) collective-permute-start(bf16[1024,363]{0,1:T(8,128)(2,1)S(1)} %pad_maximum_fusion), channel_id=1, source_target_pairs={{0,1},{1,0},{2,3},{3,2},{4,5},{5,4},{6,7},{7,6},{8,9},{9,8},{10,11... | collective-permute-start | bytes 2230280 | tf_op jit(solution)/shard_map/ppermute | solution.py:17
  5.7 0.0 copy-done
  5.7 1.6 copy.19
  7.2 0.1 copy.26
  7.3 0.6 pad_bitcast_fusion.tail
  8.0 0.0 copy-start.3
  8.0 163.5 %shard_map.122 = bf16[256,2048]{1,0:T(8,128)(2,1)} custom-call(bf16[512,1024]{1,0:T(8,128)(2,1)} %bitcast.27, bf16[4,128,1024]{2,1,0:T(8,128)(2,1)} %wb.1, bf16[128,1024]{1,0:T(8,128)(2,1)} %wd.1, bf16[16,1024]{1,0:T(8,128)(2,1)} %pad_bitcast_fusion.tail, f32[4,1024]{1,0:T(4,128)} %conv_w.1, f32[2,1024]{1,0:T(2,128)} %bias.1, f32[1,1024]{1,0:T(1,128)} %bitcast.36), custom_call_target="tpu_custom_call" | custom-call | flops 8589934592 | bytes 200000000 | tf_op jit(solution)/shard_map/pallas_call | solution.py:375
  171.5 0.0 copy-start.1
  171.5 0.1 broadcast_compare_fusion
  171.6 0.1 lt.21
  171.7 0.1 broadcast_bitcast_fusion
  171.8 0.1 reshape.67
  171.9 0.1 copy.20
  172.0 0.1 reshape_reshape.8
  172.1 1.5 multiply_reduce_fusion
  173.6 0.0 collective-permute-done
  173.7 0.4 broadcast_select_fusion.1
  174.0 0.8 copy-done.2
  174.9 0.6 fusion.4
  175.5 0.1 slice_reduce_fusion
  175.5 0.1 exponential_reduce_fusion
  175.6 0.1 dynamic-slice_select_fusion
  175.7 0.6 collective-permute-start.1
  176.3 3.1 %collective-permute-done.1 = f32[2,256]{1,0:T(2,128)S(1)} collective-permute-done((f32[2,256]{1,0:T(2,128)S(1)}, f32[2,256]{1,0:T(2,128)S(1)}, u32[]{:S(2)}, u32[]{:S(2)}) %collective-permute-start.1) | collective-permute-done | bytes 2080 | tf_op jit(solution)/shard_map/ppermute | solution.py:17
  179.4 0.1 reshape_squeeze.6
  179.5 0.1 copy.21
  179.6 0.7 reshape.69
  180.3 0.1 reshape_squeeze.7
  180.3 0.1 copy.22
  180.4 0.7 reshape.70
  (18 shorter events, 0.1 us)
Async XLA Ops:
  0.6 5.0 %copy-start = (bf16[2,256,1024]{2,1,0:T(8,128)(2,1)S(1)}, bf16[2,256,1024]{2,1,0:T(8,128)(2,1)}, u32[]{:S(2)}) copy-start(bf16[2,256,1024]{2,1,0:T(8,128)(2,1)} %param.14) | copy-start | bytes 3145732
  2.6 171.0 %collective-permute-start = (bf16[1024,363]{0,1:T(8,128)(2,1)S(1)}, bf16[1024,363]{0,1:T(8,128)(2,1)S(1)}, u32[]{:S(2)}, u32[]{:S(2)}) collective-permute-start(bf16[1024,363]{0,1:T(8,128)(2,1)S(1)} %pad_maximum_fusion), channel_id=1, source_target_pairs={{0,1},{1,0},{2,3},{3,2},{4,5},{5,4},{6,7},{7,6},{8,9},{9,8},{10,11... | collective-permute-start | bytes 2230280 | tf_op jit(solution)/shard_map/ppermute | solution.py:17
  8.0 163.6 %copy-start.4 = (s32[2]{0:T(128)S(1)}, s32[2]{0:T(128)}, u32[]{:S(2)}) copy-start(s32[2]{0:T(128)} %param.12) | copy-start | bytes 28
  8.0 163.8 %copy-start.5 = (s32[2]{0:T(128)S(1)}, s32[2]{0:T(128)}, u32[]{:S(2)}) copy-start(s32[2]{0:T(128)} %param.13) | copy-start | bytes 28
  8.0 163.9 %copy-start.3 = (s32[2,256]{1,0:T(2,128)S(1)}, s32[2,256]{1,0:T(2,128)}, u32[]{:S(2)}) copy-start(s32[2,256]{1,0:T(2,128)} %param.11) | copy-start | bytes 6148
  171.5 2.1 %copy-start.1 = (bf16[1024,362]{0,1:T(8,128)(2,1)S(1)}, bf16[1024,362]{0,1:T(8,128)(2,1)}, u32[]{:S(2)}) copy-start(bf16[1024,362]{0,1:T(8,128)(2,1)} %param.20) | copy-start | bytes 2224132
  173.6 1.2 copy-start.2
  175.7 3.6 %collective-permute-start.1 = (f32[2,256]{1,0:T(2,128)S(1)}, f32[2,256]{1,0:T(2,128)S(1)}, u32[]{:S(2)}, u32[]{:S(2)}) collective-permute-start(f32[2,256]{1,0:T(2,128)S(1)} %pad_maximum_fusion.2), channel_id=1, source_target_pairs={{0,1},{1,0},{2,3},{3,2},{4,5},{5,4},{6,7},{7,6},{8,9},{9,8},{10,11... | collective-permute-start | bytes 6152 | tf_op jit(solution)/shard_map/ppermute | solution.py:17
